TPU v7x, 8 devices: a whole 2x2x1 slice. The times are simulated.
8 devices in a mesh: dp: 1 (over z), cpo: 2 (over y), cp: 4 (over x, core).
Axes of the slice: x: 2, y: 2, z: 1, core: 2. Of those that a mesh axis runs over, the one named last changes fastest.
Arguments:
- queries: bfloat16 [4, 8192, 4, 128], P('dp', ('cpo', 'cp'))
- key_seq: bfloat16 [4, 8192, 1, 128], P('dp', ('cpo', 'cp'))
- value_seq: bfloat16 [4, 8192, 1, 128], P('dp', ('cpo', 'cp'))
- out_grad: bfloat16 [4, 8192, 4, 128], P('dp', ('cpo', 'cp'))
Outputs:
- output 1: bfloat16 [4, 8192, 4, 128], P('dp', ('cpo', 'cp'))
- output 2: bfloat16 [4, 8192, 4, 128], P('dp', ('cpo', 'cp'))
- output 3: bfloat16 [4, 8192, 1, 128], P('dp', ('cpo', 'cp'))
- output 4: bfloat16 [4, 8192, 1, 128], P('dp', ('cpo', 'cp'))
All inputs are finite; a program needn't handle non-finite values.
Results may differ from a plain program's by a relative error of at most 0.00709.
Values are sent between devices in bfloat16 or wider.
A program may use at most 1 GiB of HBM per device.

v0:
```python
import jax
import jax.numpy as jnp
from jax import lax
from jax.sharding import PartitionSpec as P


def group_heads(x_loc, kv_heads):
    batch_size, seq_len, q_heads, head_dim = x_loc.shape
    return x_loc.reshape(batch_size, seq_len, kv_heads, q_heads // kv_heads, head_dim)


def init_state(batch_size, seq_len, kv_heads, group_size, head_dim):
    stat_shape = (batch_size, kv_heads, group_size, seq_len)
    acc_out = jnp.zeros((batch_size, seq_len, kv_heads, group_size, head_dim), jnp.float32)
    return acc_out, jnp.full(stat_shape, -jnp.inf, jnp.float32), jnp.zeros(stat_shape, jnp.float32)


def fwd_update(soft_state, q_grp, k_blk, v_blk, score_scale, key_mask):
    acc_out, row_max, row_sum = soft_state
    scores = jnp.einsum('bqhgd,bkhd->bhgqk', q_grp, k_blk, preferred_element_type=jnp.float32) * score_scale
    if key_mask is not None:
        scores = jnp.where(key_mask, scores, -jnp.inf)
    new_max = jnp.maximum(row_max, scores.max(axis=-1))
    rescale = jnp.exp(row_max - new_max)
    attn_prob = jnp.exp(scores - new_max[..., None])
    row_sum = row_sum * rescale + attn_prob.sum(axis=-1)
    pv_part = jnp.einsum('bhgqk,bkhd->bqhgd', attn_prob.astype(jnp.bfloat16), v_blk, preferred_element_type=jnp.float32)
    acc_out = acc_out * jnp.transpose(rescale, (0, 3, 1, 2))[..., None] + pv_part
    return acc_out, new_max, row_sum


def finish_state(soft_state):
    acc_out, row_max, row_sum = soft_state
    out_grp = (acc_out / jnp.transpose(row_sum, (0, 3, 1, 2))[..., None]).astype(jnp.bfloat16)
    return out_grp, row_max + jnp.log(row_sum)


def grad_block(q_grp, do_grp, log_sum, row_dot, k_blk, v_blk, score_scale, key_mask):
    scores = jnp.einsum('bqhgd,bkhd->bhgqk', q_grp, k_blk, preferred_element_type=jnp.float32) * score_scale
    if key_mask is not None:
        scores = jnp.where(key_mask, scores, -jnp.inf)
    attn_prob = jnp.exp(scores - log_sum[..., None])
    dv_part = jnp.einsum('bhgqk,bqhgd->bkhd', attn_prob.astype(jnp.bfloat16), do_grp, preferred_element_type=jnp.float32)
    prob_grad = jnp.einsum('bqhgd,bkhd->bhgqk', do_grp, v_blk, preferred_element_type=jnp.float32)
    score_grad = (attn_prob * (prob_grad - row_dot[..., None])).astype(jnp.bfloat16)
    dq_part = jnp.einsum('bhgqk,bkhd->bqhgd', score_grad, k_blk, preferred_element_type=jnp.float32) * score_scale
    dk_part = jnp.einsum('bhgqk,bqhgd->bkhd', score_grad, q_grp, preferred_element_type=jnp.float32) * score_scale
    return dq_part, dk_part, dv_part


def solution(mesh):
    ctx_width = mesh.shape['cp']
    shard_count = mesh.shape['cpo'] * ctx_width
    seq_axes = ('cpo', 'cp')
    seq_spec = P('dp', seq_axes, None, None)
    shift_next = [(src_pos, (src_pos + 1) % shard_count) for src_pos in range(shard_count)]

    def pass_on(x_loc):
        return lax.ppermute(x_loc, seq_axes, shift_next)

    def local_attn(queries, key_seq, value_seq, out_grad):
        my_pos = lax.axis_index('cpo') * ctx_width + lax.axis_index('cp')
        batch_size, shard_len, q_heads, head_dim = queries.shape
        kv_heads = key_seq.shape[2]
        group_size = q_heads // kv_heads
        score_scale = head_dim ** -0.5
        q_grp = group_heads(queries, kv_heads)
        do_grp = group_heads(out_grad, kv_heads)
        row_pos = jnp.arange(shard_len)
        causal_mask = row_pos[:, None] >= row_pos[None, :]

        soft_state = init_state(batch_size, shard_len, kv_heads, group_size, head_dim)
        soft_state = fwd_update(soft_state, q_grp, key_seq, value_seq, score_scale, causal_mask)

        def fwd_step(hop_step, loop_state):
            soft_now, k_cur, v_cur = loop_state
            k_cur = pass_on(k_cur)
            v_cur = pass_on(v_cur)
            src_pos = (my_pos - hop_step) % shard_count
            soft_now = lax.cond(src_pos < my_pos, lambda same_state: fwd_update(same_state, q_grp, k_cur, v_cur, score_scale, None), lambda same_state: same_state, soft_now)
            return soft_now, k_cur, v_cur

        soft_state, _, _ = lax.fori_loop(1, shard_count, fwd_step, (soft_state, key_seq, value_seq))
        out_grp, log_sum = finish_state(soft_state)
        row_dot = jnp.einsum('bqhgd,bqhgd->bhgq', do_grp, out_grp, preferred_element_type=jnp.float32)
        dq_acc, dk_acc, dv_acc = grad_block(q_grp, do_grp, log_sum, row_dot, key_seq, value_seq, score_scale, causal_mask)

        def bwd_step(hop_step, loop_state):
            dq_now, k_cur, v_cur, dk_now, dv_now = loop_state
            k_cur = pass_on(k_cur)
            v_cur = pass_on(v_cur)
            dk_now = pass_on(dk_now)
            dv_now = pass_on(dv_now)
            src_pos = (my_pos - hop_step) % shard_count

            def add_block(grad_sums):
                dq_sum, dk_sum, dv_sum = grad_sums
                dq_part, dk_part, dv_part = grad_block(q_grp, do_grp, log_sum, row_dot, k_cur, v_cur, score_scale, None)
                return dq_sum + dq_part, dk_sum + dk_part, dv_sum + dv_part

            dq_now, dk_now, dv_now = lax.cond(src_pos < my_pos, add_block, lambda grad_sums: grad_sums, (dq_now, dk_now, dv_now))
            return dq_now, k_cur, v_cur, dk_now, dv_now

        dq_acc, _, _, dk_acc, dv_acc = lax.fori_loop(1, shard_count, bwd_step, (dq_acc, key_seq, value_seq, dk_acc, dv_acc))
        k_grad = pass_on(dk_acc.astype(jnp.bfloat16))
        v_grad = pass_on(dv_acc.astype(jnp.bfloat16))
        attn_out = out_grp.reshape(queries.shape)
        q_grad = dq_acc.astype(jnp.bfloat16).reshape(queries.shape)
        return attn_out, q_grad, k_grad, v_grad

    return jax.shard_map(local_attn, mesh=mesh, in_specs=(seq_spec, seq_spec, seq_spec, seq_spec), out_specs=(seq_spec, seq_spec, seq_spec, seq_spec), check_vma=False)
```

profile of v0, /device:TPU:0, one launch (start us, length us, event | category | flops | bytes accessed | tf_op | source)
XLA Modules:
  0.0 2427.6 jit_solution(16087147722380814240)
XLA Ops:
  4.4 27.3 %fusion.89 = (f32[4,4,1024]{2,1,0:T(4,128)S(1)}, f32[4,1,4,1024,1024]{3,4,2,0,1:T(8,128)}) fusion(bf16[4,1024,4,128]{3,2,1,0:T(4,128)(2,1)} %param.12, bf16[4,1024,1,128]{3,1,2,0:T(8,128)(2,1)} %copy.124, pred[1024,1024]{0,1:T(8,128)(4,1)S(1)} %iota_compare_fusion), kind=kOutput, calls=%fused_computation.90 | convolution fusion | flops 4345282560 | bytes 73465856 | tf_op jit(solution)/shard_map/bqhgd,bkhd->bhgqk/dot_general | solution.py:20
  31.7 21.2 fusion.48
  54.3 27.4 %bitcast_add_fusion.5 = f32[4,1024,1,4,128]{4,1,3,0,2:T(8,128)} fusion(f32[4,1024,4]{1,2,0:T(4,128)S(1)} %get-tuple-element.635, f32[4,1,4,1024,1024]{3,4,2,0,1:T(8,128)} %get-tuple-element.637, f32[4,4,1024]{2,1,0:T(4,128)S(1)} %get-tuple-element.636, bf16[4,1024,1,128]{3,1,2,0:T(8,128)(2,1)S(1)} %copy.125), kind=kOutput, calls=%fused_computation.63 | convolution fusion | flops 4330618880 | bytes 76677120 | tf_op jit(solution)/shard_map/bhgqk,bkhd->bqhgd/dot_general | solution.py:27
  89.2 638.5 %while.46 = (s32[]{:T(128)}, f32[4,1024,1,4,128]{4,1,3,0,2:T(8,128)}, f32[4,1,4,1024]{3,2,0,1:T(4,128)S(1)}, f32[4,1,4,1024]{3,2,0,1:T(4,128)S(1)}, bf16[4,1024,...) while((s32[]{:T(128)}, ...), condition=%wide.region_7.8_spmd, body=%wide.region_2.7_spmd.sunk | while | flops 8728395776 | bytes 238027200 | solution.py:83
  93.0 12.8 collective-permute-done
  105.7 11.2 collective-permute-done.1
  118.0 76.6 %collective-permute-start = (bf16[4,1024,1,128]{3,1,0,2:T(8,128)(2,1)S(1)}, bf16[4,1024,1,128]{3,1,0,2:T(8,128)(2,1)S(1)}, u32[]{:S(2)}, u32[]{:S(2)}) collective-permute-start(bf16[4,1024,1,128]{3,1,0,2:T(8,128)(2,1)S(1)} %get-tuple-element.796), channel_id=1, source_target_pairs={{0,1},{1,2},{2,3},{3,4},{4,5},{5,6},{6,7},{7,0}} | collective-permute-start | bytes 3145736 | tf_op jit(solution)/shard_map/while/body/eval_jaxpr/ppermute | solution.py:59
  197.1 10.3 collective-permute-done
  207.3 11.2 collective-permute-done.1
  221.1 80.1 %collective-permute-start.1 = (bf16[4,1024,1,128]{3,1,0,2:T(8,128)(2,1)}, bf16[4,1024,1,128]{3,1,0,2:T(8,128)(2,1)S(1)}, u32[]{:S(2)}, u32[]{:S(2)}) collective-permute-start(bf16[4,1024,1,128]{3,1,0,2:T(8,128)(2,1)} %get-tuple-element.797), channel_id=1, source_target_pairs={{0,1},{1,2},{2,3},{3,4},{4,5},{5,6},{6,7},{7,0}} | collective-permute-start | bytes 3145736 | tf_op jit(solution)/shard_map/while/body/eval_jaxpr/ppermute | solution.py:59
  301.2 7.8 collective-permute-done
  309.0 11.2 collective-permute-done.1
  327.7 82.9 %collective-permute-done = bf16[4,1024,1,128]{3,1,0,2:T(8,128)(2,1)S(1)} collective-permute-done((bf16[4,1024,1,128]{3,1,0,2:T(8,128)(2,1)S(1)}, bf16[4,1024,1,128]{3,1,0,2:T(8,128)(2,1)S(1)}, u32[]{:S(2)}, u32[]{:S(2)}) %collective-permute-start) | collective-permute-done | bytes 1048608 | tf_op jit(solution)/shard_map/while/body/eval_jaxpr/ppermute | solution.py:59
  410.6 11.2 collective-permute-done.1
  422.9 89.3 %collective-permute-done = bf16[4,1024,1,128]{3,1,0,2:T(8,128)(2,1)S(1)} collective-permute-done((bf16[4,1024,1,128]{3,1,0,2:T(8,128)(2,1)S(1)}, bf16[4,1024,1,128]{3,1,0,2:T(8,128)(2,1)S(1)}, u32[]{:S(2)}, u32[]{:S(2)}) %collective-permute-start) | collective-permute-done | bytes 1048608 | tf_op jit(solution)/shard_map/while/body/eval_jaxpr/ppermute | solution.py:59
  512.2 11.2 collective-permute-done.1
  524.5 89.3 %collective-permute-done = bf16[4,1024,1,128]{3,1,0,2:T(8,128)(2,1)S(1)} collective-permute-done((bf16[4,1024,1,128]{3,1,0,2:T(8,128)(2,1)S(1)}, bf16[4,1024,1,128]{3,1,0,2:T(8,128)(2,1)S(1)}, u32[]{:S(2)}, u32[]{:S(2)}) %collective-permute-start) | collective-permute-done | bytes 1048608 | tf_op jit(solution)/shard_map/while/body/eval_jaxpr/ppermute | solution.py:59
  613.8 11.2 collective-permute-done.1
  626.1 89.3 %collective-permute-done = bf16[4,1024,1,128]{3,1,0,2:T(8,128)(2,1)S(1)} collective-permute-done((bf16[4,1024,1,128]{3,1,0,2:T(8,128)(2,1)S(1)}, bf16[4,1024,1,128]{3,1,0,2:T(8,128)(2,1)S(1)}, u32[]{:S(2)}, u32[]{:S(2)}) %collective-permute-start) | collective-permute-done | bytes 1048608 | tf_op jit(solution)/shard_map/while/body/eval_jaxpr/ppermute | solution.py:59
  715.4 11.2 collective-permute-done.1
  727.7 36.1 %fusion.74 = f32[4,1024,1,128]{3,1,0,2:T(8,128)} fusion(bf16[4,1024,4,128]{3,2,1,0:T(4,128)(2,1)} %param.15, f32[4,1,4,1024,1024]{3,4,2,0,1:T(8,128)} %get-tuple-element.637, f32[4,4,1024]{2,1,0:T(4,128)S(1)} %bitcast.268), kind=kOutput, calls=%fused_computation.81 | convolution fusion | flops 4328521728 | bytes 73465856 | tf_op jit(solution)/shard_map/bhgqk,bqhgd->bkhd/dot_general | solution.py:43
  764.4 61.1 %fusion.63 = (f32[4,4,1024]{1,2,0:T(8,128)}, bf16[4,1024,1,4,128]{4,3,1,0,2:T(4,128)(2,1)}) fusion(bf16[4,1024,4,128]{3,2,1,0:T(4,128)(2,1)} %param.15, f32[4,1024,4]{2,1,0:T(8,128)S(1)} %copy.15, f32[4,1024,1,4,128]{4,1,3,0,2:T(8,128)} %get-tuple-element.565), kind=kLoop, calls=%fused_computation.65 | loop fusion | flops 12566528 | bytes 16908288
  827.8 36.6 %fusion.47 = bf16[4,1,4,1024,1024]{3,4,2,0,1:T(8,128)(2,1)} fusion(f32[4,1,4,1024,1024]{3,4,2,0,1:T(8,128)} %get-tuple-element.637, f32[4,4,1024]{2,1,0:T(4,128)S(1)} %copy.44, f32[4,4,1024]{2,1,0:T(4,128)S(1)} %bitcast.269, bf16[4,1024,4,128]{3,2,1,0:T(4,128)(2,1)} %param.15, bf16[4,1024,1,128]{3,1,2,0:T(8,128)(2,1)} %copy-done.1), kind=kOutput, calls=%fused_computation.46 | convolution fusion | flops 4362076160 | bytes 106037248 | tf_op jit(solution)/shard_map/bqhgd,bkhd->bhgqk/dot_general | solution.py:44
  864.4 18.6 multiply_bitcast_fusion
  883.0 16.6 fusion.73
  899.6 1372.6 %while.47 = (s32[]{:T(128)}, f32[4,1024,1,4,128]{4,1,3,0,2:T(8,128)}, bf16[4,1024,1,128]{3,1,0,2:T(8,128)(2,1)}, bf16[4,1024,1,128]{3,1,0,2:T(8,128)(2,1)}, f32[...) while((s32[]{:T(128)}, ...), condition=%wide.region_11.12_spmd, body=%wide.region_8.11_spmd.sunk | while | flops 21614821376 | bytes 401801824 | solution.py:104
  900.0 134.1 %collective-permute-done.4 = bf16[4,1024,1,128]{3,1,0,2:T(8,128)(2,1)S(1)} collective-permute-done((bf16[4,1024,1,128]{3,1,0,2:T(8,128)(2,1)}, bf16[4,1024,1,128]{3,1,0,2:T(8,128)(2,1)S(1)}, u32[]{:S(2)}, u32[]{:S(2)}) %collective-permute-start.4) | collective-permute-done | bytes 1048608 | tf_op jit(solution)/shard_map/while/body/eval_jaxpr/ppermute | solution.py:59
  1035.1 10.3 collective-permute-done.5
  1052.5 11.6 collective-permute-start.2
  1066.5 60.0 %collective-permute-start.4 = (bf16[4,1024,1,128]{3,1,0,2:T(8,128)(2,1)}, bf16[4,1024,1,128]{3,1,0,2:T(8,128)(2,1)S(1)}, u32[]{:S(2)}, u32[]{:S(2)}) collective-permute-start(bf16[4,1024,1,128]{3,1,0,2:T(8,128)(2,1)} %get-tuple-element.833), channel_id=1, source_target_pairs={{0,1},{1,2},{2,3},{3,4},{4,5},{5,6},{6,7},{7,0}} | collective-permute-start | bytes 3145736 | tf_op jit(solution)/shard_map/while/body/eval_jaxpr/ppermute | solution.py:59
  1129.9 107.4 %collective-permute-done.4 = bf16[4,1024,1,128]{3,1,0,2:T(8,128)(2,1)S(1)} collective-permute-done((bf16[4,1024,1,128]{3,1,0,2:T(8,128)(2,1)}, bf16[4,1024,1,128]{3,1,0,2:T(8,128)(2,1)S(1)}, u32[]{:S(2)}, u32[]{:S(2)}) %collective-permute-start.4) | collective-permute-done | bytes 1048608 | tf_op jit(solution)/shard_map/while/body/eval_jaxpr/ppermute | solution.py:59
  1238.3 10.3 collective-permute-done.5
  1255.7 54.1 %collective-permute-start.3 = (f32[4,1024,1,128]{3,1,0,2:T(8,128)}, f32[4,1024,1,128]{3,1,0,2:T(8,128)}, u32[]{:S(2)}, u32[]{:S(2)}) collective-permute-start(f32[4,1024,1,128]{3,1,0,2:T(8,128)} %get-tuple-element.836), channel_id=1, source_target_pairs={{0,1},{1,2},{2,3},{3,4},{4,5},{5,6},{6,7},{7,0}} | collective-permute-start | bytes 6291464 | tf_op jit(solution)/shard_map/while/body/eval_jaxpr/ppermute | solution.py:59
  1309.8 31.2 %collective-permute-start.4 = (bf16[4,1024,1,128]{3,1,0,2:T(8,128)(2,1)}, bf16[4,1024,1,128]{3,1,0,2:T(8,128)(2,1)S(1)}, u32[]{:S(2)}, u32[]{:S(2)}) collective-permute-start(bf16[4,1024,1,128]{3,1,0,2:T(8,128)(2,1)} %get-tuple-element.833), channel_id=1, source_target_pairs={{0,1},{1,2},{2,3},{3,4},{4,5},{5,6},{6,7},{7,0}} | collective-permute-start | bytes 3145736 | tf_op jit(solution)/shard_map/while/body/eval_jaxpr/ppermute | solution.py:59
  1344.4 96.2 %collective-permute-done.4 = bf16[4,1024,1,128]{3,1,0,2:T(8,128)(2,1)S(1)} collective-permute-done((bf16[4,1024,1,128]{3,1,0,2:T(8,128)(2,1)}, bf16[4,1024,1,128]{3,1,0,2:T(8,128)(2,1)S(1)}, u32[]{:S(2)}, u32[]{:S(2)}) %collective-permute-start.4) | collective-permute-done | bytes 1048608 | tf_op jit(solution)/shard_map/while/body/eval_jaxpr/ppermute | solution.py:59
  1441.6 10.3 collective-permute-done.5
  1459.0 88.7 %collective-permute-start.4 = (bf16[4,1024,1,128]{3,1,0,2:T(8,128)(2,1)}, bf16[4,1024,1,128]{3,1,0,2:T(8,128)(2,1)S(1)}, u32[]{:S(2)}, u32[]{:S(2)}) collective-permute-start(bf16[4,1024,1,128]{3,1,0,2:T(8,128)(2,1)} %get-tuple-element.833), channel_id=1, source_target_pairs={{0,1},{1,2},{2,3},{3,4},{4,5},{5,6},{6,7},{7,0}} | collective-permute-start | bytes 3145736 | tf_op jit(solution)/shard_map/while/body/eval_jaxpr/ppermute | solution.py:59
  1551.1 92.8 %collective-permute-done.4 = bf16[4,1024,1,128]{3,1,0,2:T(8,128)(2,1)S(1)} collective-permute-done((bf16[4,1024,1,128]{3,1,0,2:T(8,128)(2,1)}, bf16[4,1024,1,128]{3,1,0,2:T(8,128)(2,1)S(1)}, u32[]{:S(2)}, u32[]{:S(2)}) %collective-permute-start.4) | collective-permute-done | bytes 1048608 | tf_op jit(solution)/shard_map/while/body/eval_jaxpr/ppermute | solution.py:59
  1644.9 10.3 collective-permute-done.5
  1662.2 95.5 %collective-permute-start.5 = (bf16[4,1024,1,128]{3,1,0,2:T(8,128)(2,1)}, bf16[4,1024,1,128]{3,1,0,2:T(8,128)(2,1)S(1)}, u32[]{:S(2)}, u32[]{:S(2)}) collective-permute-start(bf16[4,1024,1,128]{3,1,0,2:T(8,128)(2,1)} %get-tuple-element.834), channel_id=1, source_target_pairs={{0,1},{1,2},{2,3},{3,4},{4,5},{5,6},{6,7},{7,0}} | collective-permute-start | bytes 3145736 | tf_op jit(solution)/shard_map/while/body/eval_jaxpr/ppermute | solution.py:59
  1757.8 89.4 %collective-permute-done.4 = bf16[4,1024,1,128]{3,1,0,2:T(8,128)(2,1)S(1)} collective-permute-done((bf16[4,1024,1,128]{3,1,0,2:T(8,128)(2,1)}, bf16[4,1024,1,128]{3,1,0,2:T(8,128)(2,1)S(1)}, u32[]{:S(2)}, u32[]{:S(2)}) %collective-permute-start.4) | collective-permute-done | bytes 1048608 | tf_op jit(solution)/shard_map/while/body/eval_jaxpr/ppermute | solution.py:59
  1848.1 10.3 collective-permute-done.5
  1865.6 184.8 %collective-permute-done.4 = bf16[4,1024,1,128]{3,1,0,2:T(8,128)(2,1)S(1)} collective-permute-done((bf16[4,1024,1,128]{3,1,0,2:T(8,128)(2,1)}, bf16[4,1024,1,128]{3,1,0,2:T(8,128)(2,1)S(1)}, u32[]{:S(2)}, u32[]{:S(2)}) %collective-permute-start.4) | collective-permute-done | bytes 1048608 | tf_op jit(solution)/shard_map/while/body/eval_jaxpr/ppermute | solution.py:59
  2051.4 10.3 collective-permute-done.5
  2068.8 184.8 %collective-permute-done.4 = bf16[4,1024,1,128]{3,1,0,2:T(8,128)(2,1)S(1)} collective-permute-done((bf16[4,1024,1,128]{3,1,0,2:T(8,128)(2,1)}, bf16[4,1024,1,128]{3,1,0,2:T(8,128)(2,1)S(1)}, u32[]{:S(2)}, u32[]{:S(2)}) %collective-permute-start.4) | collective-permute-done | bytes 1048608 | tf_op jit(solution)/shard_map/while/body/eval_jaxpr/ppermute | solution.py:59
  2254.6 10.3 collective-permute-done.5
  2285.2 128.8 %collective-permute-done.6 = bf16[4,1024,1,128]{3,1,2,0:T(8,128)(2,1)S(1)} collective-permute-done((bf16[4,1024,1,128]{3,1,2,0:T(8,128)(2,1)S(1)}, bf16[4,1024,1,128]{3,1,2,0:T(8,128)(2,1)S(1)}, u32[]{:S(2)}, u32[]{:S(2)}) %collective-permute-start.6) | collective-permute-done | bytes 1048608 | tf_op jit(solution)/shard_map/ppermute | solution.py:59
  2414.0 11.2 collective-permute-done.7
  (126 shorter events, 121.1 us)
Async XLA Ops:
  4.1 77.5 %copy-start.1 = (bf16[4,1024,1,128]{3,1,2,0:T(8,128)(2,1)}, bf16[4,1024,1,128]{3,1,2,0:T(8,128)(2,1)S(1)}, u32[]{:S(2)}) copy-start(bf16[4,1024,1,128]{3,1,2,0:T(8,128)(2,1)S(1)} %copy.125) | copy-start | bytes 3145732
  89.5 16.2 collective-permute-start
  90.4 26.6 %collective-permute-start.1 = (bf16[4,1024,1,128]{3,1,0,2:T(8,128)(2,1)}, bf16[4,1024,1,128]{3,1,0,2:T(8,128)(2,1)S(1)}, u32[]{:S(2)}, u32[]{:S(2)}) collective-permute-start(bf16[4,1024,1,128]{3,1,0,2:T(8,128)(2,1)} %get-tuple-element.797), channel_id=1, source_target_pairs={{0,1},{1,2},{2,3},{3,4},{4,5},{5,6},{6,7},{7,0}} | collective-permute-start | bytes 3145736 | tf_op jit(solution)/shard_map/while/body/eval_jaxpr/ppermute | solution.py:59
  118.0 89.3 %collective-permute-start = (bf16[4,1024,1,128]{3,1,0,2:T(8,128)(2,1)S(1)}, bf16[4,1024,1,128]{3,1,0,2:T(8,128)(2,1)S(1)}, u32[]{:S(2)}, u32[]{:S(2)}) collective-permute-start(bf16[4,1024,1,128]{3,1,0,2:T(8,128)(2,1)S(1)} %get-tuple-element.796), channel_id=1, source_target_pairs={{0,1},{1,2},{2,3},{3,4},{4,5},{5,6},{6,7},{7,0}} | collective-permute-start | bytes 3145736 | tf_op jit(solution)/shard_map/while/body/eval_jaxpr/ppermute | solution.py:59
  194.6 24.0 collective-permute-start.1
  219.6 89.3 %collective-permute-start = (bf16[4,1024,1,128]{3,1,0,2:T(8,128)(2,1)S(1)}, bf16[4,1024,1,128]{3,1,0,2:T(8,128)(2,1)S(1)}, u32[]{:S(2)}, u32[]{:S(2)}) collective-permute-start(bf16[4,1024,1,128]{3,1,0,2:T(8,128)(2,1)S(1)} %get-tuple-element.796), channel_id=1, source_target_pairs={{0,1},{1,2},{2,3},{3,4},{4,5},{5,6},{6,7},{7,0}} | collective-permute-start | bytes 3145736 | tf_op jit(solution)/shard_map/while/body/eval_jaxpr/ppermute | solution.py:59
  221.1 99.1 %collective-permute-start.1 = (bf16[4,1024,1,128]{3,1,0,2:T(8,128)(2,1)}, bf16[4,1024,1,128]{3,1,0,2:T(8,128)(2,1)S(1)}, u32[]{:S(2)}, u32[]{:S(2)}) collective-permute-start(bf16[4,1024,1,128]{3,1,0,2:T(8,128)(2,1)} %get-tuple-element.797), channel_id=1, source_target_pairs={{0,1},{1,2},{2,3},{3,4},{4,5},{5,6},{6,7},{7,0}} | collective-permute-start | bytes 3145736 | tf_op jit(solution)/shard_map/while/body/eval_jaxpr/ppermute | solution.py:59
  321.2 89.3 %collective-permute-start = (bf16[4,1024,1,128]{3,1,0,2:T(8,128)(2,1)S(1)}, bf16[4,1024,1,128]{3,1,0,2:T(8,128)(2,1)S(1)}, u32[]{:S(2)}, u32[]{:S(2)}) collective-permute-start(bf16[4,1024,1,128]{3,1,0,2:T(8,128)(2,1)S(1)} %get-tuple-element.796), channel_id=1, source_target_pairs={{0,1},{1,2},{2,3},{3,4},{4,5},{5,6},{6,7},{7,0}} | collective-permute-start | bytes 3145736 | tf_op jit(solution)/shard_map/while/body/eval_jaxpr/ppermute | solution.py:59
  325.2 96.6 %collective-permute-start.1 = (bf16[4,1024,1,128]{3,1,0,2:T(8,128)(2,1)}, bf16[4,1024,1,128]{3,1,0,2:T(8,128)(2,1)S(1)}, u32[]{:S(2)}, u32[]{:S(2)}) collective-permute-start(bf16[4,1024,1,128]{3,1,0,2:T(8,128)(2,1)} %get-tuple-element.797), channel_id=1, source_target_pairs={{0,1},{1,2},{2,3},{3,4},{4,5},{5,6},{6,7},{7,0}} | collective-permute-start | bytes 3145736 | tf_op jit(solution)/shard_map/while/body/eval_jaxpr/ppermute | solution.py:59
  422.9 89.3 %collective-permute-start = (bf16[4,1024,1,128]{3,1,0,2:T(8,128)(2,1)S(1)}, bf16[4,1024,1,128]{3,1,0,2:T(8,128)(2,1)S(1)}, u32[]{:S(2)}, u32[]{:S(2)}) collective-permute-start(bf16[4,1024,1,128]{3,1,0,2:T(8,128)(2,1)S(1)} %get-tuple-element.796), channel_id=1, source_target_pairs={{0,1},{1,2},{2,3},{3,4},{4,5},{5,6},{6,7},{7,0}} | collective-permute-start | bytes 3145736 | tf_op jit(solution)/shard_map/while/body/eval_jaxpr/ppermute | solution.py:59
  422.9 100.6 %collective-permute-start.1 = (bf16[4,1024,1,128]{3,1,0,2:T(8,128)(2,1)}, bf16[4,1024,1,128]{3,1,0,2:T(8,128)(2,1)S(1)}, u32[]{:S(2)}, u32[]{:S(2)}) collective-permute-start(bf16[4,1024,1,128]{3,1,0,2:T(8,128)(2,1)} %get-tuple-element.797), channel_id=1, source_target_pairs={{0,1},{1,2},{2,3},{3,4},{4,5},{5,6},{6,7},{7,0}} | collective-permute-start | bytes 3145736 | tf_op jit(solution)/shard_map/while/body/eval_jaxpr/ppermute | solution.py:59
  524.5 89.3 %collective-permute-start = (bf16[4,1024,1,128]{3,1,0,2:T(8,128)(2,1)S(1)}, bf16[4,1024,1,128]{3,1,0,2:T(8,128)(2,1)S(1)}, u32[]{:S(2)}, u32[]{:S(2)}) collective-permute-start(bf16[4,1024,1,128]{3,1,0,2:T(8,128)(2,1)S(1)} %get-tuple-element.796), channel_id=1, source_target_pairs={{0,1},{1,2},{2,3},{3,4},{4,5},{5,6},{6,7},{7,0}} | collective-permute-start | bytes 3145736 | tf_op jit(solution)/shard_map/while/body/eval_jaxpr/ppermute | solution.py:59
  524.5 100.6 %collective-permute-start.1 = (bf16[4,1024,1,128]{3,1,0,2:T(8,128)(2,1)}, bf16[4,1024,1,128]{3,1,0,2:T(8,128)(2,1)S(1)}, u32[]{:S(2)}, u32[]{:S(2)}) collective-permute-start(bf16[4,1024,1,128]{3,1,0,2:T(8,128)(2,1)} %get-tuple-element.797), channel_id=1, source_target_pairs={{0,1},{1,2},{2,3},{3,4},{4,5},{5,6},{6,7},{7,0}} | collective-permute-start | bytes 3145736 | tf_op jit(solution)/shard_map/while/body/eval_jaxpr/ppermute | solution.py:59
  626.1 89.3 %collective-permute-start = (bf16[4,1024,1,128]{3,1,0,2:T(8,128)(2,1)S(1)}, bf16[4,1024,1,128]{3,1,0,2:T(8,128)(2,1)S(1)}, u32[]{:S(2)}, u32[]{:S(2)}) collective-permute-start(bf16[4,1024,1,128]{3,1,0,2:T(8,128)(2,1)S(1)} %get-tuple-element.796), channel_id=1, source_target_pairs={{0,1},{1,2},{2,3},{3,4},{4,5},{5,6},{6,7},{7,0}} | collective-permute-start | bytes 3145736 | tf_op jit(solution)/shard_map/while/body/eval_jaxpr/ppermute | solution.py:59
  626.1 100.6 %collective-permute-start.1 = (bf16[4,1024,1,128]{3,1,0,2:T(8,128)(2,1)}, bf16[4,1024,1,128]{3,1,0,2:T(8,128)(2,1)S(1)}, u32[]{:S(2)}, u32[]{:S(2)}) collective-permute-start(bf16[4,1024,1,128]{3,1,0,2:T(8,128)(2,1)} %get-tuple-element.797), channel_id=1, source_target_pairs={{0,1},{1,2},{2,3},{3,4},{4,5},{5,6},{6,7},{7,0}} | collective-permute-start | bytes 3145736 | tf_op jit(solution)/shard_map/while/body/eval_jaxpr/ppermute | solution.py:59
  864.4 18.6 copy-start.2
  899.8 146.6 %collective-permute-start.2 = (f32[4,1024,1,128]{3,1,0,2:T(8,128)}, f32[4,1024,1,128]{3,1,0,2:T(8,128)}, u32[]{:S(2)}, u32[]{:S(2)}) collective-permute-start(f32[4,1024,1,128]{3,1,0,2:T(8,128)} %get-tuple-element.835), channel_id=1, source_target_pairs={{0,1},{1,2},{2,3},{3,4},{4,5},{5,6},{6,7},{7,0}} | collective-permute-start | bytes 6291464 | tf_op jit(solution)/shard_map/while/body/eval_jaxpr/ppermute | solution.py:59
  899.8 146.5 %collective-permute-start.3 = (f32[4,1024,1,128]{3,1,0,2:T(8,128)}, f32[4,1024,1,128]{3,1,0,2:T(8,128)}, u32[]{:S(2)}, u32[]{:S(2)}) collective-permute-start(f32[4,1024,1,128]{3,1,0,2:T(8,128)} %get-tuple-element.836), channel_id=1, source_target_pairs={{0,1},{1,2},{2,3},{3,4},{4,5},{5,6},{6,7},{7,0}} | collective-permute-start | bytes 6291464 | tf_op jit(solution)/shard_map/while/body/eval_jaxpr/ppermute | solution.py:59
  899.9 134.2 %collective-permute-start.4 = (bf16[4,1024,1,128]{3,1,0,2:T(8,128)(2,1)}, bf16[4,1024,1,128]{3,1,0,2:T(8,128)(2,1)S(1)}, u32[]{:S(2)}, u32[]{:S(2)}) collective-permute-start(bf16[4,1024,1,128]{3,1,0,2:T(8,128)(2,1)} %get-tuple-element.833), channel_id=1, source_target_pairs={{0,1},{1,2},{2,3},{3,4},{4,5},{5,6},{6,7},{7,0}} | collective-permute-start | bytes 3145736 | tf_op jit(solution)/shard_map/while/body/eval_jaxpr/ppermute | solution.py:59
  899.9 145.4 %collective-permute-start.5 = (bf16[4,1024,1,128]{3,1,0,2:T(8,128)(2,1)}, bf16[4,1024,1,128]{3,1,0,2:T(8,128)(2,1)S(1)}, u32[]{:S(2)}, u32[]{:S(2)}) collective-permute-start(bf16[4,1024,1,128]{3,1,0,2:T(8,128)(2,1)} %get-tuple-element.834), channel_id=1, source_target_pairs={{0,1},{1,2},{2,3},{3,4},{4,5},{5,6},{6,7},{7,0}} | collective-permute-start | bytes 3145736 | tf_op jit(solution)/shard_map/while/body/eval_jaxpr/ppermute | solution.py:59
  1052.5 197.2 %collective-permute-start.2 = (f32[4,1024,1,128]{3,1,0,2:T(8,128)}, f32[4,1024,1,128]{3,1,0,2:T(8,128)}, u32[]{:S(2)}, u32[]{:S(2)}) collective-permute-start(f32[4,1024,1,128]{3,1,0,2:T(8,128)} %get-tuple-element.835), channel_id=1, source_target_pairs={{0,1},{1,2},{2,3},{3,4},{4,5},{5,6},{6,7},{7,0}} | collective-permute-start | bytes 6291464 | tf_op jit(solution)/shard_map/while/body/eval_jaxpr/ppermute | solution.py:59
  1064.0 185.6 %collective-permute-start.3 = (f32[4,1024,1,128]{3,1,0,2:T(8,128)}, f32[4,1024,1,128]{3,1,0,2:T(8,128)}, u32[]{:S(2)}, u32[]{:S(2)}) collective-permute-start(f32[4,1024,1,128]{3,1,0,2:T(8,128)} %get-tuple-element.836), channel_id=1, source_target_pairs={{0,1},{1,2},{2,3},{3,4},{4,5},{5,6},{6,7},{7,0}} | collective-permute-start | bytes 6291464 | tf_op jit(solution)/shard_map/while/body/eval_jaxpr/ppermute | solution.py:59
  1066.5 170.8 %collective-permute-start.4 = (bf16[4,1024,1,128]{3,1,0,2:T(8,128)(2,1)}, bf16[4,1024,1,128]{3,1,0,2:T(8,128)(2,1)S(1)}, u32[]{:S(2)}, u32[]{:S(2)}) collective-permute-start(bf16[4,1024,1,128]{3,1,0,2:T(8,128)(2,1)} %get-tuple-element.833), channel_id=1, source_target_pairs={{0,1},{1,2},{2,3},{3,4},{4,5},{5,6},{6,7},{7,0}} | collective-permute-start | bytes 3145736 | tf_op jit(solution)/shard_map/while/body/eval_jaxpr/ppermute | solution.py:59
  1126.5 122.1 %collective-permute-start.5 = (bf16[4,1024,1,128]{3,1,0,2:T(8,128)(2,1)}, bf16[4,1024,1,128]{3,1,0,2:T(8,128)(2,1)S(1)}, u32[]{:S(2)}, u32[]{:S(2)}) collective-permute-start(bf16[4,1024,1,128]{3,1,0,2:T(8,128)(2,1)} %get-tuple-element.834), channel_id=1, source_target_pairs={{0,1},{1,2},{2,3},{3,4},{4,5},{5,6},{6,7},{7,0}} | collective-permute-start | bytes 3145736 | tf_op jit(solution)/shard_map/while/body/eval_jaxpr/ppermute | solution.py:59
  1255.7 197.2 %collective-permute-start.2 = (f32[4,1024,1,128]{3,1,0,2:T(8,128)}, f32[4,1024,1,128]{3,1,0,2:T(8,128)}, u32[]{:S(2)}, u32[]{:S(2)}) collective-permute-start(f32[4,1024,1,128]{3,1,0,2:T(8,128)} %get-tuple-element.835), channel_id=1, source_target_pairs={{0,1},{1,2},{2,3},{3,4},{4,5},{5,6},{6,7},{7,0}} | collective-permute-start | bytes 6291464 | tf_op jit(solution)/shard_map/while/body/eval_jaxpr/ppermute | solution.py:59
  1255.7 197.2 %collective-permute-start.3 = (f32[4,1024,1,128]{3,1,0,2:T(8,128)}, f32[4,1024,1,128]{3,1,0,2:T(8,128)}, u32[]{:S(2)}, u32[]{:S(2)}) collective-permute-start(f32[4,1024,1,128]{3,1,0,2:T(8,128)} %get-tuple-element.836), channel_id=1, source_target_pairs={{0,1},{1,2},{2,3},{3,4},{4,5},{5,6},{6,7},{7,0}} | collective-permute-start | bytes 6291464 | tf_op jit(solution)/shard_map/while/body/eval_jaxpr/ppermute | solution.py:59
  1309.8 130.8 %collective-permute-start.4 = (bf16[4,1024,1,128]{3,1,0,2:T(8,128)(2,1)}, bf16[4,1024,1,128]{3,1,0,2:T(8,128)(2,1)S(1)}, u32[]{:S(2)}, u32[]{:S(2)}) collective-permute-start(bf16[4,1024,1,128]{3,1,0,2:T(8,128)(2,1)} %get-tuple-element.833), channel_id=1, source_target_pairs={{0,1},{1,2},{2,3},{3,4},{4,5},{5,6},{6,7},{7,0}} | collective-permute-start | bytes 3145736 | tf_op jit(solution)/shard_map/while/body/eval_jaxpr/ppermute | solution.py:59
  1341.0 110.8 %collective-permute-start.5 = (bf16[4,1024,1,128]{3,1,0,2:T(8,128)(2,1)}, bf16[4,1024,1,128]{3,1,0,2:T(8,128)(2,1)S(1)}, u32[]{:S(2)}, u32[]{:S(2)}) collective-permute-start(bf16[4,1024,1,128]{3,1,0,2:T(8,128)(2,1)} %get-tuple-element.834), channel_id=1, source_target_pairs={{0,1},{1,2},{2,3},{3,4},{4,5},{5,6},{6,7},{7,0}} | collective-permute-start | bytes 3145736 | tf_op jit(solution)/shard_map/while/body/eval_jaxpr/ppermute | solution.py:59
  1459.0 197.2 %collective-permute-start.2 = (f32[4,1024,1,128]{3,1,0,2:T(8,128)}, f32[4,1024,1,128]{3,1,0,2:T(8,128)}, u32[]{:S(2)}, u32[]{:S(2)}) collective-permute-start(f32[4,1024,1,128]{3,1,0,2:T(8,128)} %get-tuple-element.835), channel_id=1, source_target_pairs={{0,1},{1,2},{2,3},{3,4},{4,5},{5,6},{6,7},{7,0}} | collective-permute-start | bytes 6291464 | tf_op jit(solution)/shard_map/while/body/eval_jaxpr/ppermute | solution.py:59
  1459.0 197.2 %collective-permute-start.3 = (f32[4,1024,1,128]{3,1,0,2:T(8,128)}, f32[4,1024,1,128]{3,1,0,2:T(8,128)}, u32[]{:S(2)}, u32[]{:S(2)}) collective-permute-start(f32[4,1024,1,128]{3,1,0,2:T(8,128)} %get-tuple-element.836), channel_id=1, source_target_pairs={{0,1},{1,2},{2,3},{3,4},{4,5},{5,6},{6,7},{7,0}} | collective-permute-start | bytes 6291464 | tf_op jit(solution)/shard_map/while/body/eval_jaxpr/ppermute | solution.py:59
  1459.0 184.9 %collective-permute-start.4 = (bf16[4,1024,1,128]{3,1,0,2:T(8,128)(2,1)}, bf16[4,1024,1,128]{3,1,0,2:T(8,128)(2,1)S(1)}, u32[]{:S(2)}, u32[]{:S(2)}) collective-permute-start(bf16[4,1024,1,128]{3,1,0,2:T(8,128)(2,1)} %get-tuple-element.833), channel_id=1, source_target_pairs={{0,1},{1,2},{2,3},{3,4},{4,5},{5,6},{6,7},{7,0}} | collective-permute-start | bytes 3145736 | tf_op jit(solution)/shard_map/while/body/eval_jaxpr/ppermute | solution.py:59
  1547.7 107.4 %collective-permute-start.5 = (bf16[4,1024,1,128]{3,1,0,2:T(8,128)(2,1)}, bf16[4,1024,1,128]{3,1,0,2:T(8,128)(2,1)S(1)}, u32[]{:S(2)}, u32[]{:S(2)}) collective-permute-start(bf16[4,1024,1,128]{3,1,0,2:T(8,128)(2,1)} %get-tuple-element.834), channel_id=1, source_target_pairs={{0,1},{1,2},{2,3},{3,4},{4,5},{5,6},{6,7},{7,0}} | collective-permute-start | bytes 3145736 | tf_op jit(solution)/shard_map/while/body/eval_jaxpr/ppermute | solution.py:59
  1662.2 197.2 %collective-permute-start.2 = (f32[4,1024,1,128]{3,1,0,2:T(8,128)}, f32[4,1024,1,128]{3,1,0,2:T(8,128)}, u32[]{:S(2)}, u32[]{:S(2)}) collective-permute-start(f32[4,1024,1,128]{3,1,0,2:T(8,128)} %get-tuple-element.835), channel_id=1, source_target_pairs={{0,1},{1,2},{2,3},{3,4},{4,5},{5,6},{6,7},{7,0}} | collective-permute-start | bytes 6291464 | tf_op jit(solution)/shard_map/while/body/eval_jaxpr/ppermute | solution.py:59
  1662.2 197.2 %collective-permute-start.3 = (f32[4,1024,1,128]{3,1,0,2:T(8,128)}, f32[4,1024,1,128]{3,1,0,2:T(8,128)}, u32[]{:S(2)}, u32[]{:S(2)}) collective-permute-start(f32[4,1024,1,128]{3,1,0,2:T(8,128)} %get-tuple-element.836), channel_id=1, source_target_pairs={{0,1},{1,2},{2,3},{3,4},{4,5},{5,6},{6,7},{7,0}} | collective-permute-start | bytes 6291464 | tf_op jit(solution)/shard_map/while/body/eval_jaxpr/ppermute | solution.py:59
  1662.2 184.9 %collective-permute-start.4 = (bf16[4,1024,1,128]{3,1,0,2:T(8,128)(2,1)}, bf16[4,1024,1,128]{3,1,0,2:T(8,128)(2,1)S(1)}, u32[]{:S(2)}, u32[]{:S(2)}) collective-permute-start(bf16[4,1024,1,128]{3,1,0,2:T(8,128)(2,1)} %get-tuple-element.833), channel_id=1, source_target_pairs={{0,1},{1,2},{2,3},{3,4},{4,5},{5,6},{6,7},{7,0}} | collective-permute-start | bytes 3145736 | tf_op jit(solution)/shard_map/while/body/eval_jaxpr/ppermute | solution.py:59
  1662.2 196.1 %collective-permute-start.5 = (bf16[4,1024,1,128]{3,1,0,2:T(8,128)(2,1)}, bf16[4,1024,1,128]{3,1,0,2:T(8,128)(2,1)S(1)}, u32[]{:S(2)}, u32[]{:S(2)}) collective-permute-start(bf16[4,1024,1,128]{3,1,0,2:T(8,128)(2,1)} %get-tuple-element.834), channel_id=1, source_target_pairs={{0,1},{1,2},{2,3},{3,4},{4,5},{5,6},{6,7},{7,0}} | collective-permute-start | bytes 3145736 | tf_op jit(solution)/shard_map/while/body/eval_jaxpr/ppermute | solution.py:59
  1865.5 197.2 %collective-permute-start.2 = (f32[4,1024,1,128]{3,1,0,2:T(8,128)}, f32[4,1024,1,128]{3,1,0,2:T(8,128)}, u32[]{:S(2)}, u32[]{:S(2)}) collective-permute-start(f32[4,1024,1,128]{3,1,0,2:T(8,128)} %get-tuple-element.835), channel_id=1, source_target_pairs={{0,1},{1,2},{2,3},{3,4},{4,5},{5,6},{6,7},{7,0}} | collective-permute-start | bytes 6291464 | tf_op jit(solution)/shard_map/while/body/eval_jaxpr/ppermute | solution.py:59
  1865.5 197.2 %collective-permute-start.3 = (f32[4,1024,1,128]{3,1,0,2:T(8,128)}, f32[4,1024,1,128]{3,1,0,2:T(8,128)}, u32[]{:S(2)}, u32[]{:S(2)}) collective-permute-start(f32[4,1024,1,128]{3,1,0,2:T(8,128)} %get-tuple-element.836), channel_id=1, source_target_pairs={{0,1},{1,2},{2,3},{3,4},{4,5},{5,6},{6,7},{7,0}} | collective-permute-start | bytes 6291464 | tf_op jit(solution)/shard_map/while/body/eval_jaxpr/ppermute | solution.py:59
  1865.5 184.9 %collective-permute-start.4 = (bf16[4,1024,1,128]{3,1,0,2:T(8,128)(2,1)}, bf16[4,1024,1,128]{3,1,0,2:T(8,128)(2,1)S(1)}, u32[]{:S(2)}, u32[]{:S(2)}) collective-permute-start(bf16[4,1024,1,128]{3,1,0,2:T(8,128)(2,1)} %get-tuple-element.833), channel_id=1, source_target_pairs={{0,1},{1,2},{2,3},{3,4},{4,5},{5,6},{6,7},{7,0}} | collective-permute-start | bytes 3145736 | tf_op jit(solution)/shard_map/while/body/eval_jaxpr/ppermute | solution.py:59
  1865.5 196.1 %collective-permute-start.5 = (bf16[4,1024,1,128]{3,1,0,2:T(8,128)(2,1)}, bf16[4,1024,1,128]{3,1,0,2:T(8,128)(2,1)S(1)}, u32[]{:S(2)}, u32[]{:S(2)}) collective-permute-start(bf16[4,1024,1,128]{3,1,0,2:T(8,128)(2,1)} %get-tuple-element.834), channel_id=1, source_target_pairs={{0,1},{1,2},{2,3},{3,4},{4,5},{5,6},{6,7},{7,0}} | collective-permute-start | bytes 3145736 | tf_op jit(solution)/shard_map/while/body/eval_jaxpr/ppermute | solution.py:59
  2068.8 197.2 %collective-permute-start.2 = (f32[4,1024,1,128]{3,1,0,2:T(8,128)}, f32[4,1024,1,128]{3,1,0,2:T(8,128)}, u32[]{:S(2)}, u32[]{:S(2)}) collective-permute-start(f32[4,1024,1,128]{3,1,0,2:T(8,128)} %get-tuple-element.835), channel_id=1, source_target_pairs={{0,1},{1,2},{2,3},{3,4},{4,5},{5,6},{6,7},{7,0}} | collective-permute-start | bytes 6291464 | tf_op jit(solution)/shard_map/while/body/eval_jaxpr/ppermute | solution.py:59
  2068.8 197.2 %collective-permute-start.3 = (f32[4,1024,1,128]{3,1,0,2:T(8,128)}, f32[4,1024,1,128]{3,1,0,2:T(8,128)}, u32[]{:S(2)}, u32[]{:S(2)}) collective-permute-start(f32[4,1024,1,128]{3,1,0,2:T(8,128)} %get-tuple-element.836), channel_id=1, source_target_pairs={{0,1},{1,2},{2,3},{3,4},{4,5},{5,6},{6,7},{7,0}} | collective-permute-start | bytes 6291464 | tf_op jit(solution)/shard_map/while/body/eval_jaxpr/ppermute | solution.py:59
  2068.8 184.9 %collective-permute-start.4 = (bf16[4,1024,1,128]{3,1,0,2:T(8,128)(2,1)}, bf16[4,1024,1,128]{3,1,0,2:T(8,128)(2,1)S(1)}, u32[]{:S(2)}, u32[]{:S(2)}) collective-permute-start(bf16[4,1024,1,128]{3,1,0,2:T(8,128)(2,1)} %get-tuple-element.833), channel_id=1, source_target_pairs={{0,1},{1,2},{2,3},{3,4},{4,5},{5,6},{6,7},{7,0}} | collective-permute-start | bytes 3145736 | tf_op jit(solution)/shard_map/while/body/eval_jaxpr/ppermute | solution.py:59
  2068.8 196.1 %collective-permute-start.5 = (bf16[4,1024,1,128]{3,1,0,2:T(8,128)(2,1)}, bf16[4,1024,1,128]{3,1,0,2:T(8,128)(2,1)S(1)}, u32[]{:S(2)}, u32[]{:S(2)}) collective-permute-start(bf16[4,1024,1,128]{3,1,0,2:T(8,128)(2,1)} %get-tuple-element.834), channel_id=1, source_target_pairs={{0,1},{1,2},{2,3},{3,4},{4,5},{5,6},{6,7},{7,0}} | collective-permute-start | bytes 3145736 | tf_op jit(solution)/shard_map/while/body/eval_jaxpr/ppermute | solution.py:59
  2274.0 140.0 %collective-permute-start.6 = (bf16[4,1024,1,128]{3,1,2,0:T(8,128)(2,1)S(1)}, bf16[4,1024,1,128]{3,1,2,0:T(8,128)(2,1)S(1)}, u32[]{:S(2)}, u32[]{:S(2)}) collective-permute-start(bf16[4,1024,1,128]{3,1,2,0:T(8,128)(2,1)S(1)} %bitcast_convert_fusion.1), channel_id=1, source_target_pairs={{0,1},{1,2},{2,3},{3,4},{4,5},{5,6},{6,7},{7,0}} | collective-permute-start | bytes 3145736 | tf_op jit(solution)/shard_map/ppermute | solution.py:59
  2275.7 149.5 %collective-permute-start.7 = (bf16[4,1024,1,128]{3,1,2,0:T(8,128)(2,1)S(1)}, bf16[4,1024,1,128]{3,1,2,0:T(8,128)(2,1)S(1)}, u32[]{:S(2)}, u32[]{:S(2)}) collective-permute-start(bf16[4,1024,1,128]{3,1,2,0:T(8,128)(2,1)S(1)} %bitcast_convert_fusion), channel_id=1, source_target_pairs={{0,1},{1,2},{2,3},{3,4},{4,5},{5,6},{6,7},{7,0}} | collective-permute-start | bytes 3145736 | tf_op jit(solution)/shard_map/ppermute | solution.py:59
where the time goes:
time: 2440 us; the launch traced here: 2430 us
  waiting for transfers between devices  1560 us (64%)
  starting transfers between devices  525 us (22%)
  matrix products  163 us (7%)
  other arithmetic  90.3 us (4%)
  local copies, waits for them, and re-layouts  86.2 us (4%)
    ppermute x44, waiting for transfers between devices, pass_on(): return lax.ppermute(x_loc, seq_axes, shift_next)  1560 us
    ppermute x44, starting transfers between devices, pass_on(): return lax.ppermute(x_loc, seq_axes, shift_next)  525 us
    while x42, local copies, waits for them, and re-layouts  63.8 us
    unnamed x1, other arithmetic  61.1 us
  transfers between devices with their start and end apart: 44, of which 30 were waited for; matrix products, arithmetic and copies ran while one was open for 1% of the time, Pallas kernels for 0%

commit v1 on v0

v1 whole, which is shorter than its diff:
```python
import functools
import math

import jax
import jax.numpy as jnp
from jax import lax
from jax.experimental import pallas as pl
from jax.experimental.pallas import tpu as pltpu
from jax.sharding import PartitionSpec as P

F32 = jnp.float32
BF16 = jnp.bfloat16
N_DEV = 8
N_SEQ = 4
SHARD = 1024
HEAD = 128
ROWS = 2 * SHARD
CHUNK = 1024
HALF = 512
SCALE = HEAD ** -0.5
LOG2_SCALE = SCALE * math.log2(math.e)
NT = (((1,), (1,)), ((), ()))
NN = (((1,), (0,)), ((), ()))
MESH_ID = pl.DeviceIdType.MESH


def dot(lhs, rhs, dims):
    return lax.dot_general(lhs, rhs, dims, preferred_element_type=F32)


def causal(scores, key_start, token_start, fill):
    key_pos = key_start + lax.broadcasted_iota(jnp.int32, scores.shape, 0)
    row_tok = token_start + lax.broadcasted_iota(jnp.int32, scores.shape, 1) // 2
    return jnp.where(key_pos <= row_tok, scores, fill)


def attn_kernel(q_in, k_in, v_in, do_in, o_out, dq_out, dkv_out,
                q_buf, k_buf, v_buf, do_buf, kt_buf, vt_buf, acc_t, dkv_acc, stage, part, dkv_stage, row_m, row_l,
                in_send, in_recv, out_send, out_recv, loc_sem):
    y_pos = lax.axis_index('cpo')
    b_pos = lax.axis_index('cp')
    x_pos = b_pos // 2
    core = b_pos % 2
    chip = y_pos * 2 + x_pos
    me = chip * 2 + core

    def dev(shard):
        return (lax.axis_index('dp'), shard // 4, shard % 4)

    def by_code(code):
        return ((y_pos + code // 4) % 2) * 4 + ((x_pos + (code // 2) % 2) % 2) * 2 + (core + code % 2) % 2

    def code_of(shard):
        return ((y_pos + shard // 4) % 2) * 4 + ((x_pos + (shard // 2) % 2) % 2) * 2 + (core + shard % 2) % 2

    def arrival(n):
        is3 = (n // 3) % 2 * (1 - n // 4)
        is4 = n // 4 - n // 5
        return n + is3 - is4

    def departure(n):
        u = n // 2
        mid = (u * (3 - u)) // 2
        rel = 3 * ((3 - u) // 3) + mid * (1 + n % 2)
        cidx = (1 - mid) * (n % 2) + mid * (u - 1)
        return ((y_pos + rel // 2) % 2) * 4 + ((x_pos + rel % 2) % 2) * 2 + cidx

    srcs = (k_in, v_in, q_in, do_in)
    bufs = (k_buf, v_buf, q_buf, do_buf)

    def in_copy(what, code):
        to = by_code(code)
        src = srcs[what].at[to // 2] if what < 2 else srcs[what].at[to // 2, to % 2]
        return pltpu.make_async_remote_copy(
            src_ref=src, dst_ref=bufs[what].at[me], send_sem=in_send.at[what, code], recv_sem=in_recv.at[what, code],
            device_id=dev(to), device_id_type=MESH_ID)

    def own_copy(what):
        src = srcs[what].at[chip] if what < 2 else srcs[what].at[chip, core]
        return pltpu.make_async_copy(src, bufs[what].at[me], loc_sem.at[what])

    barrier = pltpu.get_barrier_semaphore()
    for code in range(1, N_DEV):
        pl.semaphore_signal(barrier, inc=1, device_id=dev(by_code(code)), device_id_type=MESH_ID)
    for what in range(4):
        own_copy(what).start()
    pl.semaphore_wait(barrier, N_DEV - 1)

    for code in range(1, N_DEV):
        for what in range(3):
            in_copy(what, code).start()
    for code in range(1, N_DEV):
        in_copy(3, code).start()

    def fwd_scores(i, row0, j, nkeys):
        return dot(k_buf[j, pl.ds(0, nkeys), :], q_buf[i, pl.ds(row0, CHUNK), :], NT)

    def fwd_diag(i):
        for c in range(2):
            rows = pl.ds(c * CHUNK, CHUNK)
            nkeys = (c + 1) * HALF
            s_t = causal(fwd_scores(i, c * CHUNK, i, nkeys), 0, c * HALF, -jnp.inf)
            mx = jnp.max(s_t, axis=0, keepdims=True)
            p_t = jnp.exp2((s_t - mx) * LOG2_SCALE)
            row_m[i, :, rows] = mx
            row_l[i, :, rows] = jnp.sum(p_t, axis=0, keepdims=True)
            acc_t[i, :, rows] = dot(vt_buf[i, :, pl.ds(0, nkeys)], p_t.astype(BF16), NN)

    def fwd_full(i, j):
        s_all = [fwd_scores(i, c * CHUNK, j, SHARD) for c in range(2)]
        for c in range(2):
            rows = pl.ds(c * CHUNK, CHUNK)
            s_t = s_all[c]
            old = row_m[i, :, rows]
            mx = jnp.maximum(old, jnp.max(s_t, axis=0, keepdims=True))
            keep = jnp.exp2((old - mx) * LOG2_SCALE)
            p_t = jnp.exp2((s_t - mx) * LOG2_SCALE)
            row_m[i, :, rows] = mx
            row_l[i, :, rows] = row_l[i, :, rows] * keep + jnp.sum(p_t, axis=0, keepdims=True)
            acc_t[i, :, rows] = acc_t[i, :, rows] * keep + dot(vt_buf[j], p_t.astype(BF16), NN)

    def fwd_shard(n, first):
        code = arrival(n)
        new = by_code(code)
        if first:
            for what in range(3):
                own_copy(what).wait()
        else:
            for what in range(3):
                in_copy(what, code).wait_recv()
        kt_buf[new] = k_buf[new].T
        vt_buf[new] = v_buf[new].T
        fwd_diag(new)
        if not first:
            def pair(t, carry):
                old = by_code(arrival(t))
                fwd_full(jnp.maximum(new, old), jnp.minimum(new, old))
                return carry
            lax.fori_loop(0, n, pair, 0)

    fwd_shard(0, True)

    def fwd_loop(n, carry):
        fwd_shard(n, False)
        return carry
    lax.fori_loop(1, N_DEV, fwd_loop, 0)

    def out_copy(what, shard, code):
        src = dkv_stage.at[shard] if what == 2 else stage.at[shard]
        dst = dkv_out.at[core, chip] if what == 2 else (o_out, dq_out)[what].at[chip, core]
        return pltpu.make_async_remote_copy(
            src_ref=src, dst_ref=dst, send_sem=out_send.at[what, code], recv_sem=out_recv.at[what, code],
            device_id=dev(shard), device_id_type=MESH_ID)

    def out_own(what):
        src = dkv_stage.at[me] if what == 2 else stage.at[me]
        dst = dkv_out.at[core, chip] if what == 2 else (o_out, dq_out)[what].at[chip, core]
        return pltpu.make_async_copy(src, dst, loc_sem.at[4 + what])

    def start_out(what, shard):
        code = code_of(shard)

        @pl.when(code == 0)
        def _():
            out_own(what).start()

        @pl.when(code > 0)
        def _():
            out_copy(what, shard, code).start()

    def wait_out(what, shard):
        code = code_of(shard)

        @pl.when(code == 0)
        def _():
            out_own(what).wait()

        @pl.when(code > 0)
        def _():
            out_copy(what, shard, code).wait_send()

    own_copy(3).wait()

    def fin_loop(n, carry):
        shard = departure(n)
        code = code_of(shard)

        @pl.when(code > 0)
        def _():
            in_copy(3, code).wait_recv()

        for c in range(2):
            rows = pl.ds(c * CHUNK, CHUNK)
            total = row_l[shard, :, rows]
            o_t = (acc_t[shard, :, rows] * (1.0 / total)).astype(BF16)
            o_rows = o_t.T
            stage[shard, rows, :] = o_rows
            row_m[shard, :, rows] = row_m[shard, :, rows] * LOG2_SCALE + jnp.log2(total)
            prod = o_rows.astype(F32) * do_buf[shard, rows, :].astype(F32)
            row_l[shard, :, rows] = jnp.sum(prod.T, axis=0, keepdims=True)
            acc_t[shard, :, rows] = jnp.zeros((HEAD, CHUNK), F32)
        dkv_acc[0, shard] = jnp.zeros((SHARD, HEAD), F32)
        dkv_acc[1, shard] = jnp.zeros((SHARD, HEAD), F32)
        start_out(0, shard)
        return carry
    lax.fori_loop(0, N_DEV, fin_loop, 0)

    def bwd_block(i, row0, nrow, j, key0, nkeys, masked, token0):
        keys = pl.ds(key0, nkeys)
        k_blk = k_buf[j, keys, :]
        v_blk = v_buf[j, keys, :]
        s_all, dp_all = [], []
        starts = [row0 + c * HALF for c in range(nrow)]
        for r0 in starts:
            s_all.append(dot(k_blk, q_buf[i, pl.ds(r0, HALF), :], NT))
            dp_all.append(dot(v_blk, do_buf[i, pl.ds(r0, HALF), :], NT))
        p_all, ds_all = [], []
        for c, r0 in enumerate(starts):
            rows = pl.ds(r0, HALF)
            p_t = jnp.exp2(s_all[c] * LOG2_SCALE - row_m[i, :, rows])
            if masked:
                p_t = causal(p_t, key0, token0 + c * (HALF // 2), 0.0)
            p_all.append(p_t.astype(BF16))
            ds_all.append((p_t * (dp_all[c] - row_l[i, :, rows])).astype(BF16))
        dv_new, dk_new = None, None
        for c, r0 in enumerate(starts):
            rows = pl.ds(r0, HALF)
            dv_c = dot(p_all[c], do_buf[i, rows, :], NN)
            dk_c = dot(ds_all[c], q_buf[i, rows, :], NN)
            dv_new = dv_c if dv_new is None else dv_new + dv_c
            dk_new = dk_c if dk_new is None else dk_new + dk_c
        dkv_acc[0, j, keys, :] += dv_new
        dkv_acc[1, j, keys, :] += dk_new
        for c, r0 in enumerate(starts):
            rows = pl.ds(r0, HALF)
            acc_t[i, :, rows] += dot(kt_buf[j, :, keys], ds_all[c], NN)

    def bwd_diag(i):
        bwd_block(i, 0, 2, i, 0, HALF, True, 0)
        bwd_block(i, CHUNK, 2, i, 0, HALF, False, HALF)
        bwd_block(i, CHUNK, 2, i, HALF, HALF, True, HALF)

    def bwd_full(i, j):
        def chunk(c, carry):
            bwd_block(i, pl.multiple_of(c * CHUNK, CHUNK), 2, j, 0, SHARD, False, 0)
            return carry
        lax.fori_loop(0, 2, chunk, 0)

    def part_copy(shard):
        return pltpu.make_async_remote_copy(
            src_ref=dkv_acc.at[1 - core, shard], dst_ref=part.at[shard], send_sem=out_send.at[3, shard],
            recv_sem=out_recv.at[3, shard], device_id=dev(chip * 2 + 1 - core), device_id_type=MESH_ID)

    def finish_dkv(shard):
        part_copy(shard).wait_recv()
        factor = jnp.where(core == 0, 1.0, SCALE).astype(F32)
        dkv_stage[shard] = ((dkv_acc[core, shard] + part[shard]) * factor).astype(BF16)
        start_out(2, shard)

    def bwd_loop(n, carry):
        shard = departure(n)
        bwd_diag(shard)

        def pair(t, carry):
            other = departure(t)
            bwd_full(jnp.maximum(shard, other), jnp.minimum(shard, other))
            return carry
        lax.fori_loop(n + 1, N_DEV, pair, 0)
        part_copy(shard).start()
        wait_out(0, shard)
        for c in range(2):
            rows = pl.ds(c * CHUNK, CHUNK)
            stage[shard, rows, :] = (acc_t[shard, :, rows] * SCALE).astype(BF16).T
        start_out(1, shard)

        @pl.when(n > 0)
        def _():
            finish_dkv(departure(n - 1))
        return carry
    lax.fori_loop(0, N_DEV, bwd_loop, 0)
    finish_dkv(departure(N_DEV - 1))

    for code in range(1, N_DEV):
        for what in range(4):
            in_copy(what, code).wait_send()
    for n in range(N_DEV):
        shard = departure(n)
        part_copy(shard).wait_send()
        wait_out(1, shard)
        wait_out(2, shard)
    for code in range(1, N_DEV):
        for what in range(3):
            out_copy(what, by_code(code), code).wait_recv()


def local_attn(queries, key_seq, value_seq, out_grad):
    def split(x):
        x = x.reshape(N_SEQ, SHARD, 2, 2, HEAD)
        return jnp.transpose(x, (0, 2, 1, 3, 4)).reshape(N_SEQ, 2, ROWS, HEAD)

    def join(x):
        x = x.reshape(N_SEQ, 2, SHARD, 2, HEAD)
        return jnp.transpose(x, (0, 2, 1, 3, 4)).reshape(N_SEQ, SHARD, 4, HEAD)

    any_spec = pl.BlockSpec(memory_space=pl.ANY)
    o_x, dq_x, dkv_x = pl.pallas_call(
        attn_kernel,
        out_shape=(
            jax.ShapeDtypeStruct((N_SEQ, 2, ROWS, HEAD), BF16),
            jax.ShapeDtypeStruct((N_SEQ, 2, ROWS, HEAD), BF16),
            jax.ShapeDtypeStruct((2, N_SEQ, SHARD, HEAD), BF16),
        ),
        in_specs=[any_spec] * 4,
        out_specs=[any_spec] * 3,
        scratch_shapes=[
            pltpu.VMEM((N_DEV, ROWS, HEAD), BF16),
            pltpu.VMEM((N_DEV, SHARD, HEAD), BF16),
            pltpu.VMEM((N_DEV, SHARD, HEAD), BF16),
            pltpu.VMEM((N_DEV, ROWS, HEAD), BF16),
            pltpu.VMEM((N_DEV, HEAD, SHARD), BF16),
            pltpu.VMEM((N_DEV, HEAD, SHARD), BF16),
            pltpu.VMEM((N_DEV, HEAD, ROWS), F32),
            pltpu.VMEM((2, N_DEV, SHARD, HEAD), F32),
            pltpu.VMEM((N_DEV, ROWS, HEAD), BF16),
            pltpu.VMEM((N_DEV, SHARD, HEAD), F32),
            pltpu.VMEM((N_DEV, SHARD, HEAD), BF16),
            pltpu.VMEM((N_DEV, 1, ROWS), F32),
            pltpu.VMEM((N_DEV, 1, ROWS), F32),
            pltpu.SemaphoreType.DMA((4, N_DEV)),
            pltpu.SemaphoreType.DMA((4, N_DEV)),
            pltpu.SemaphoreType.DMA((4, N_DEV)),
            pltpu.SemaphoreType.DMA((4, N_DEV)),
            pltpu.SemaphoreType.DMA((7,)),
        ],
        compiler_params=pltpu.CompilerParams(
            collective_id=0, has_side_effects=True, vmem_limit_bytes=67043328),
        name='ctx_attn',
    )(split(queries), key_seq.reshape(N_SEQ, SHARD, HEAD), value_seq.reshape(N_SEQ, SHARD, HEAD), split(out_grad))
    k_grad = dkv_x[1].reshape(key_seq.shape)
    v_grad = dkv_x[0].reshape(value_seq.shape)
    return join(o_x), join(dq_x), k_grad, v_grad


def solution(mesh):
    seq_spec = P('dp', ('cpo', 'cp'), None, None)
    return jax.shard_map(local_attn, mesh=mesh, in_specs=(seq_spec,) * 4, out_specs=(seq_spec,) * 4, check_vma=False)
```

time: 2440 us -> 385 us (0.16)
  waiting for transfers between devices: 1560 us -> 0 us
  starting transfers between devices: 525 us -> 0 us
  Pallas kernels: 0 us -> 358 us
  matrix products: 163 us -> 0 us
  other arithmetic: 90.3 us -> 0 us
  local copies, waits for them, and re-layouts: 86.2 us -> 26.3 us
    ppermute x44 -> x0, waiting for transfers between devices: 1560 us -> none  [pass_on(): return lax.ppermute(x_loc, seq_axes, shift_next)]
    ppermute x44 -> x0, starting transfers between devices: 525 us -> none  [pass_on(): return lax.ppermute(x_loc, seq_axes, shift_next)]
    pallas_call x0 -> x1, Pallas kernels: none -> 358 us  [local_attn(): pl.pallas_call(attn_kernel, out_shape=(jax.ShapeDtypeStruct((N_SEQ, 2, RO...]
    dot_general x6 -> x0, matrix products: 163 us -> none  [the longest x1 36.6 us: grad_block(): jnp.einsum('bqhgd,bkhd->bhgqk', do_grp, v_blk, preferred_element_type=jnp...]
    while x42 -> x0, local copies, waits for them, and re-layouts: 63.8 us -> none
    unnamed x1 -> x0, other arithmetic: 61.1 us -> none
  transfers between devices with their start and end apart: 44 -> 0, of which waited for: 30 -> 0; matrix products, arithmetic and copies ran while one was open for 1% -> 0% of each run, Pallas kernels for 0% -> 0%
where the time goes in v1:
time: 385 us
  Pallas kernels  358 us (93%)
  local copies, waits for them, and re-layouts  26.3 us (7%)
    pallas_call x1, Pallas kernels, local_attn(): pl.pallas_call(attn_kernel, out_shape=(jax.ShapeDtypeStruct((N_SEQ, 2, RO...  358 us
    reshape x2, local copies, waits for them, and re-layouts, split(): x = x.reshape(N_SEQ, SHARD, 2, 2, HEAD)  12.7 us
    transpose x2, local copies, waits for them, and re-layouts, join(): return jnp.transpose(x, (0, 2, 1, 3, 4)).reshape(N_SEQ, SHARD, 4, HEAD)  12.1 us

profile of v1, /device:TPU:0, one launch (start us, length us, event | category | flops | bytes accessed | tf_op | source)
XLA Modules:
  0.0 385.1 jit_solution(6400210576939007872)
XLA Ops:
  0.6 0.0 copy-start
  0.6 7.6 %copy.8 = bf16[4,1024,2,2,128]{4,3,1,2,0:T(2,128)(2,1)} copy(bf16[4,1024,2,2,128]{4,3,2,1,0:T(2,128)(2,1)} %bitcast.28) | data formatting | bytes 8388608 | tf_op jit(solution)/shard_map/reshape | solution.py:298
  8.2 0.0 copy-done
  8.2 5.1 %copy.9 = bf16[4,1024,2,2,128]{4,3,1,2,0:T(2,128)(2,1)} copy(bf16[4,1024,2,2,128]{4,3,2,1,0:T(2,128)(2,1)S(1)} %bitcast.29) | data formatting | bytes 8388608 | tf_op jit(solution)/shard_map/reshape | solution.py:298
  13.3 358.1 %ctx_attn.1 = (bf16[4,2,2048,128]{3,2,1,0:T(8,128)(2,1)}, bf16[4,2,2048,128]{3,2,1,0:T(8,128)(2,1)}, bf16[2,4,1024,128]{3,2,1,0:T(8,128)(2,1)}) custom-call(bf16[4,2,2048,128]{3,2,1,0:T(8,128)(2,1)} %bitcast.26, bf16[4,1024,128]{2,1,0:T(8,128)(2,1)} %bitcast.34, bf16[4,1024,128]{2,1,0:T(8,128)(2,1)} %bitcast.35, bf16[4,2,2048,128]{3,2,1,0:T(8,128)(2,1)} %bitcast.27), custom_call_target="tpu_custom_call" | custom-call | tf_op jit(solution)/shard_map/ctx_attn/pallas_call | solution.py:306
  371.4 0.0 copy-start.1
  371.5 7.2 %copy.10 = bf16[4,1024,2,2,128]{4,3,2,1,0:T(2,128)(2,1)} copy(bf16[4,1024,2,2,128]{4,3,1,2,0:T(2,128)(2,1)} %bitcast.33) | data formatting | bytes 8388608 | tf_op jit(solution)/shard_map/transpose | solution.py:303
  378.7 0.0 copy-done.1
  378.7 0.0 copy-start.2
  378.7 4.9 %copy.11 = bf16[4,1024,2,2,128]{4,3,2,1,0:T(2,128)(2,1)} copy(bf16[4,1024,2,2,128]{4,3,1,2,0:T(2,128)(2,1)S(1)} %bitcast.32) | data formatting | bytes 8388608 | tf_op jit(solution)/shard_map/transpose | solution.py:303
  383.6 0.0 copy-done.2
  383.6 1.5 slice_bitcast_fusion
Async XLA Ops:
  0.6 7.6 %copy-start = (bf16[4,1024,4,128]{3,2,1,0:T(4,128)(2,1)S(1)}, bf16[4,1024,4,128]{3,2,1,0:T(4,128)(2,1)}, u32[]{:S(2)}) copy-start(bf16[4,1024,4,128]{3,2,1,0:T(4,128)(2,1)} %param.7) | copy-start | bytes 12582916
  371.4 7.2 %copy-start.1 = (bf16[4,2,2048,128]{3,2,1,0:T(8,128)(2,1)S(1)}, bf16[4,2,2048,128]{3,2,1,0:T(8,128)(2,1)}, u32[]{:S(2)}) copy-start(bf16[4,2,2048,128]{3,2,1,0:T(8,128)(2,1)} %get-tuple-element.8) | copy-start | bytes 12582916
  378.7 4.9 %copy-start.2 = (bf16[2,4,1024,128]{3,2,1,0:T(8,128)(2,1)S(1)}, bf16[2,4,1024,128]{3,2,1,0:T(8,128)(2,1)}, u32[]{:S(2)}) copy-start(bf16[2,4,1024,128]{3,2,1,0:T(8,128)(2,1)} %get-tuple-element.9) | copy-start | bytes 6291460

commit v2 on v1

v2 whole, which is shorter than its diff:
```python
import functools
import math

import jax
import jax.numpy as jnp
from jax import lax
from jax.experimental import pallas as pl
from jax.experimental.pallas import tpu as pltpu
from jax.sharding import PartitionSpec as P

F32 = jnp.float32
BF16 = jnp.bfloat16
N_DEV = 8
N_SEQ = 4
SHARD = 1024
HEAD = 128
ROWS = 2 * SHARD
SUB = 512
N_SUB = ROWS // SUB
SCALE = HEAD ** -0.5
LOG2_SCALE = SCALE * math.log2(math.e)
NN = (((1,), (0,)), ((), ()))
MESH_ID = pl.DeviceIdType.MESH


def dot(lhs, rhs, dims):
    return lax.dot_general(lhs, rhs, dims, preferred_element_type=F32)


def causal(scores, key_start, token_start, fill):
    key_pos = key_start + lax.broadcasted_iota(jnp.int32, scores.shape, 0)
    row_tok = token_start + lax.broadcasted_iota(jnp.int32, scores.shape, 1) // 2
    return jnp.where(key_pos <= row_tok, scores, fill)


def attn_kernel(q_in, k_in, v_in, do_in, o_out, dq_out, dkv_out,
                q_land, do_land, kv_buf, q_t, do_t, kv_t, acc_t, dkv_t, stage, part, p_rows, ds_rows, s_buf, row_m, row_l,
                in_send, in_recv, fwd_send, fwd_recv, out_send, out_recv, loc_sem):
    y_pos = lax.axis_index('cpo')
    b_pos = lax.axis_index('cp')
    x_pos = b_pos // 2
    core = b_pos % 2
    chip = y_pos * 2 + x_pos
    me = chip * 2 + core
    mate = chip * 2 + 1 - core

    def dev(shard):
        return (lax.axis_index('dp'), shard // 4, shard % 4)

    def chip_at(rel):
        return ((y_pos + rel // 2) % 2) * 2 + (x_pos + rel % 2) % 2

    def by_code(code):
        return chip_at(code // 2) * 2 + (core + code % 2) % 2

    def arrival(n):
        u = n // 2
        own = (3 - u) // 3
        rel = (u * (3 - u)) // 2 * (1 + n % 2) + 3 * (n // 6)
        late = n // 4 - n // 6
        cidx = n % 2 + late * (1 - 2 * (n % 2))
        return chip_at(rel) * 2 + own * ((core + n) % 2) + (1 - own) * cidx

    def departure(n):
        u = n // 2
        mid = (u * (3 - u)) // 2
        rel = 3 * ((3 - u) // 3) + mid * (1 + n % 2)
        cidx = (1 - mid) * (n % 2) + mid * (u - 1)
        return chip_at(rel) * 2 + cidx

    kv_in = (k_in, v_in)

    def kv_copy(what, to, source):
        return pltpu.make_async_remote_copy(
            src_ref=kv_in[what].at[to // 2], dst_ref=kv_buf.at[what, source],
            send_sem=in_send.at[what, to], recv_sem=in_recv.at[what, source], device_id=dev(to), device_id_type=MESH_ID)

    def kv_direct(source):
        return pltpu.make_async_remote_copy(
            src_ref=k_in.at[0], dst_ref=kv_buf.at[core, source],
            send_sem=in_send.at[core, source], recv_sem=in_recv.at[core, source], device_id=dev(mate), device_id_type=MESH_ID)

    def kv_pass(source, what):
        return pltpu.make_async_remote_copy(
            src_ref=kv_buf.at[what, source], dst_ref=kv_buf.at[what, source],
            send_sem=fwd_send.at[source], recv_sem=fwd_recv.at[source], device_id=dev(mate), device_id_type=MESH_ID)

    def row_copy(what, to, source):
        src, dst = (q_in, q_land) if what == 2 else (do_in, do_land)
        return pltpu.make_async_remote_copy(
            src_ref=src.at[to // 2, :, to % 2], dst_ref=dst.at[source],
            send_sem=in_send.at[what, to], recv_sem=in_recv.at[what, source], device_id=dev(to), device_id_type=MESH_ID)

    def own_copy(what):
        if what < 2:
            return pltpu.make_async_copy(kv_in[what].at[chip], kv_buf.at[what, me], loc_sem.at[what])
        src, dst = (q_in, q_land) if what == 2 else (do_in, do_land)
        return pltpu.make_async_copy(src.at[chip, :, core], dst.at[me], loc_sem.at[what])

    barrier = pltpu.get_barrier_semaphore()
    for code in range(1, N_DEV):
        pl.semaphore_signal(barrier, inc=1, device_id=dev(by_code(code)), device_id_type=MESH_ID)
    for what in range(4):
        own_copy(what).start()
    pl.semaphore_wait(barrier, N_DEV - 1)

    for what in range(2):
        kv_copy(what, mate, me).start()
    row_copy(2, mate, me).start()
    def send_kvq(rel):
        for what in range(2):
            kv_copy(what, chip_at(rel) * 2 + what, me).start()
        for cidx in range(2):
            row_copy(2, chip_at(rel) * 2 + cidx, me).start()

    def send_do():
        row_copy(3, mate, me).start()
        for rel in (3, 1, 2):
            for cidx in range(2):
                row_copy(3, chip_at(rel) * 2 + cidx, me).start()

    send_kvq(1 + core)

    def turn(land, dst, shard):
        for c in range(N_SUB):
            blk = land[shard, pl.ds(c * SUB // 2, SUB // 2)].reshape(SUB, HEAD)
            dst[shard, :, pl.ds(c * SUB, SUB)] = blk.T

    def fwd_diag(i):
        for c in range(N_SUB):
            rows = pl.ds(c * SUB, SUB)
            nkeys = (c + 1) * (SUB // 2)
            s_t = dot(kv_buf[0, i, pl.ds(0, nkeys), :], q_t[i, :, rows], NN)
            s_t = causal(s_t, 0, c * (SUB // 2), -jnp.inf)
            mx = jnp.max(s_t, axis=0, keepdims=True)
            p_t = jnp.exp2((s_t - mx) * LOG2_SCALE)
            row_m[i, :, rows] = mx
            row_l[i, :, rows] = jnp.sum(p_t, axis=0, keepdims=True)
            acc_t[i, :, rows] = dot(kv_t[i, :, pl.ds(0, nkeys)], p_t.astype(BF16), NN)

    def fwd_pairs(new, n):
        def place(step):
            old = arrival(step // N_SUB)
            return jnp.maximum(new, old), jnp.minimum(new, old), pl.ds(pl.multiple_of(step % N_SUB * SUB, SUB), SUB)

        def scores(step):
            i, j, rows = place(step)
            return dot(kv_buf[0, j], q_t[i, :, rows], NN)

        def softmax(step, slot):
            i, j, rows = place(step)
            s_t = s_buf[slot]
            old = row_m[i, :, rows]
            mx = jnp.maximum(old, jnp.max(s_t, axis=0, keepdims=True))
            keep = jnp.exp2((old - mx) * LOG2_SCALE)
            row_m[i, :, rows] = mx
            total, out = row_l[i, :, rows] * keep, acc_t[i, :, rows] * keep
            for k0 in range(0, SHARD, SHARD // 2):
                p_t = jnp.exp2((s_t[k0:k0 + SHARD // 2] - mx) * LOG2_SCALE)
                total += jnp.sum(p_t, axis=0, keepdims=True)
                out += dot(kv_t[j, :, pl.ds(k0, SHARD // 2)], p_t.astype(BF16), NN)
            row_l[i, :, rows] = total
            acc_t[i, :, rows] = out

        def two(step, carry):
            for slot in range(2):
                now = step * 2 + slot
                s_buf[1 - slot] = scores(jnp.minimum(now + 1, n * N_SUB - 1))
                softmax(now, slot)
            return carry

        @pl.when(n > 0)
        def _():
            s_buf[0] = scores(0)
            lax.fori_loop(0, n * (N_SUB // 2), two, 0)

    def fwd_loop(n, carry):
        new = arrival(n)

        @pl.when(n == 0)
        def _():
            for what in range(3):
                own_copy(what).wait()

        @pl.when(n == 1)
        def _():
            for what in range(2):
                kv_copy(what, mate, new).wait_recv()

        @pl.when(n > 0)
        def _():
            row_copy(2, mate, new).wait_recv()

        turn(q_land, q_t, new)

        @pl.when(n > 1)
        def _():
            kv_pass(new, 1 - core).wait_recv()

        kv_t[new] = kv_buf[1, new].T
        fwd_diag(new)

        fwd_pairs(new, n)

        @pl.when((n > 0) & (n < N_DEV - 1))
        def _():
            following = (arrival(n + 1))
            kv_direct(following).wait_recv()
            kv_pass(following, core).start()

        @pl.when(n == 1)
        def _():
            send_kvq(2 - core)

        @pl.when(n == 3 + core)
        def _():
            send_kvq(3)

        @pl.when(n == 5 - core)
        def _():
            send_do()
        return carry
    lax.fori_loop(0, N_DEV, fwd_loop, 0)
    for n in range(2, N_DEV):
        kv_pass(arrival(n), core).wait_send()

    def out_refs(what, shard):
        if what == 2:
            return kv_buf.at[0, shard], dkv_out.at[core, chip]
        return stage.at[shard], (o_out, dq_out)[what].at[chip, core]

    def out_copy(what, shard, source):
        src, dst = out_refs(what, shard)
        return pltpu.make_async_remote_copy(
            src_ref=src, dst_ref=dst, send_sem=out_send.at[what, shard], recv_sem=out_recv.at[what, source],
            device_id=dev(shard), device_id_type=MESH_ID)

    def out_own(what):
        src, dst = out_refs(what, me)
        return pltpu.make_async_copy(src, dst, loc_sem.at[4 + what])

    def start_out(what, shard):
        @pl.when(shard == me)
        def _():
            out_own(what).start()

        @pl.when(shard != me)
        def _():
            out_copy(what, shard, me).start()

    def wait_out(what, shard):
        @pl.when(shard == me)
        def _():
            out_own(what).wait()

        @pl.when(shard != me)
        def _():
            out_copy(what, shard, me).wait_send()

    def finish_fwd(shard):
        @pl.when(shard == me)
        def _():
            own_copy(3).wait()

        @pl.when(shard != me)
        def _():
            row_copy(3, mate, shard).wait_recv()

        turn(do_land, do_t, shard)
        kv_t[shard] = kv_buf[0, shard].T
        for c in range(N_SUB):
            rows = pl.ds(c * SUB, SUB)
            total = row_l[shard, :, rows]
            o_c = (acc_t[shard, :, rows] * (1.0 / total)).astype(BF16)
            stage[shard, rows, :] = o_c.T
            row_m[shard, :, rows] = row_m[shard, :, rows] * LOG2_SCALE + jnp.log2(total)
            row_l[shard, :, rows] = jnp.sum(o_c.astype(F32) * do_t[shard, :, rows].astype(F32), axis=0, keepdims=True)
            acc_t[shard, :, rows] = jnp.zeros((HEAD, SUB), F32)
        dkv_t[0, shard] = jnp.zeros((HEAD, SHARD), F32)
        dkv_t[1, shard] = jnp.zeros((HEAD, SHARD), F32)
        start_out(0, shard)

    def bwd_block(i, row0, j, nkeys, token0, slot):
        keys = pl.ds(0, nkeys)
        rows = pl.ds(row0, SUB)
        s_t = dot(kv_buf[0, j, keys, :], q_t[i, :, rows], NN)
        dp_t = dot(kv_buf[1, j, keys, :], do_t[i, :, rows], NN)
        p_t = jnp.exp2(s_t * LOG2_SCALE - row_m[i, :, rows])
        if token0 is not None:
            p_t = causal(p_t, 0, token0, 0.0)
        ds_t = (p_t * (dp_t - row_l[i, :, rows])).astype(BF16)
        p_rows[slot, :, keys] = p_t.astype(BF16).T
        ds_rows[slot, :, keys] = ds_t.T
        acc_t[i, :, rows] += dot(kv_t[j, :, keys], ds_t, NN)
        dkv_t[0, j, :, keys] += dot(do_t[i, :, rows], p_rows[slot, :, keys], NN)
        dkv_t[1, j, :, keys] += dot(q_t[i, :, rows], ds_rows[slot, :, keys], NN)

    def bwd_diag(i):
        for c in range(N_SUB):
            bwd_block(i, c * SUB, i, (c + 1) * (SUB // 2), c * (SUB // 2), c % 2)

    def bwd_full(i, j):
        def two(c, carry):
            for slot in range(2):
                bwd_block(i, pl.multiple_of(c * (2 * SUB) + slot * SUB, SUB), j, SHARD, None, slot)
            return carry
        lax.fori_loop(0, N_SUB // 2, two, 0)

    def part_copy(shard):
        return pltpu.make_async_remote_copy(
            src_ref=dkv_t.at[1 - core, shard], dst_ref=part.at[shard], send_sem=out_send.at[3, shard],
            recv_sem=out_recv.at[3, shard], device_id=dev(mate), device_id_type=MESH_ID)

    def finish_dkv(shard):
        part_copy(shard).wait_recv()
        factor = jnp.where(core == 0, 1.0, SCALE).astype(F32)
        kv_buf[0, shard] = ((dkv_t[core, shard] + part[shard]) * factor).astype(BF16).T
        start_out(2, shard)

    finish_fwd(departure(0))

    def bwd_loop(n, carry):
        shard = departure(n)
        bwd_diag(shard)

        def pair(t, carry):
            other = departure(t)

            @pl.when(n == 0)
            def _():
                finish_fwd(other)

            bwd_full(jnp.maximum(shard, other), jnp.minimum(shard, other))
            return carry
        lax.fori_loop(n + 1, N_DEV, pair, 0)
        part_copy(shard).start()
        wait_out(0, shard)
        for c in range(N_SUB):
            rows = pl.ds(c * SUB, SUB)
            stage[shard, rows, :] = (acc_t[shard, :, rows] * SCALE).astype(BF16).T
        start_out(1, shard)

        @pl.when(n > 0)
        def _():
            finish_dkv(departure(n - 1))
        return carry
    lax.fori_loop(0, N_DEV, bwd_loop, 0)
    finish_dkv(departure(N_DEV - 1))

    for what in range(2):
        kv_copy(what, mate, me).wait_send()
        for rel in (1, 2, 3):
            kv_copy(what, chip_at(rel) * 2 + what, me).wait_send()
    for code in range(1, N_DEV):
        for what in (2, 3):
            row_copy(what, by_code(code), me).wait_send()
    for n in range(N_DEV):
        shard = departure(n)
        part_copy(shard).wait_send()
        wait_out(1, shard)
        wait_out(2, shard)
    for code in range(1, N_DEV):
        source = by_code(code)
        for what in range(3):
            out_copy(what, source, source).wait_recv()


def local_attn(queries, key_seq, value_seq, out_grad):
    def join(x):
        x = x.reshape(N_SEQ, 2, SHARD, 2, HEAD)
        return jnp.transpose(x, (0, 2, 1, 3, 4)).reshape(N_SEQ, SHARD, 4, HEAD)

    any_spec = pl.BlockSpec(memory_space=pl.ANY)
    o_x, dq_x, dkv_x = pl.pallas_call(
        attn_kernel,
        out_shape=(
            jax.ShapeDtypeStruct((N_SEQ, 2, ROWS, HEAD), BF16),
            jax.ShapeDtypeStruct((N_SEQ, 2, ROWS, HEAD), BF16),
            jax.ShapeDtypeStruct((2, N_SEQ, SHARD, HEAD), BF16),
        ),
        in_specs=[any_spec] * 4,
        out_specs=[any_spec] * 3,
        scratch_shapes=[
            pltpu.VMEM((N_DEV, SHARD, 2, HEAD), BF16),
            pltpu.VMEM((N_DEV, SHARD, 2, HEAD), BF16),
            pltpu.VMEM((2, N_DEV, SHARD, HEAD), BF16),
            pltpu.VMEM((N_DEV, HEAD, ROWS), BF16),
            pltpu.VMEM((N_DEV, HEAD, ROWS), BF16),
            pltpu.VMEM((N_DEV, HEAD, SHARD), BF16),
            pltpu.VMEM((N_DEV, HEAD, ROWS), F32),
            pltpu.VMEM((2, N_DEV, HEAD, SHARD), F32),
            pltpu.VMEM((N_DEV, ROWS, HEAD), BF16),
            pltpu.VMEM((N_DEV, HEAD, SHARD), F32),
            pltpu.VMEM((2, SUB, SHARD), BF16),
            pltpu.VMEM((2, SUB, SHARD), BF16),
            pltpu.VMEM((2, SHARD, SUB), F32),
            pltpu.VMEM((N_DEV, 1, ROWS), F32),
            pltpu.VMEM((N_DEV, 1, ROWS), F32),
            pltpu.SemaphoreType.DMA((4, N_DEV)),
            pltpu.SemaphoreType.DMA((4, N_DEV)),
            pltpu.SemaphoreType.DMA((N_DEV,)),
            pltpu.SemaphoreType.DMA((N_DEV,)),
            pltpu.SemaphoreType.DMA((4, N_DEV)),
            pltpu.SemaphoreType.DMA((4, N_DEV)),
            pltpu.SemaphoreType.DMA((7,)),
        ],
        compiler_params=pltpu.CompilerParams(
            collective_id=0, has_side_effects=True, vmem_limit_bytes=67043328),
        name='ctx_attn',
    )(queries.reshape(N_SEQ, SHARD, 2, 2, HEAD), key_seq.reshape(N_SEQ, SHARD, HEAD),
      value_seq.reshape(N_SEQ, SHARD, HEAD), out_grad.reshape(N_SEQ, SHARD, 2, 2, HEAD))
    k_grad = dkv_x[1].reshape(key_seq.shape)
    v_grad = dkv_x[0].reshape(value_seq.shape)
    return join(o_x), join(dq_x), k_grad, v_grad


def solution(mesh):
    seq_spec = P('dp', ('cpo', 'cp'), None, None)
    return jax.shard_map(local_attn, mesh=mesh, in_specs=(seq_spec,) * 4, out_specs=(seq_spec,) * 4, check_vma=False)
```

time: 385 us -> 307 us (0.80)
  Pallas kernels: 358 us -> 292 us
  local copies, waits for them, and re-layouts: 26.3 us -> 13.6 us
    pallas_call x1, Pallas kernels: 358 us -> 292 us  [local_attn(): pl.pallas_call(attn_kernel, out_shape=(jax.ShapeDtypeStruct((N_SEQ, 2, RO...]
    reshape x2 -> x0, local copies, waits for them, and re-layouts: 12.7 us -> none  [split(): x = x.reshape(N_SEQ, SHARD, 2, 2, HEAD)]
where the time goes in v2:
time: 307 us; the launch traced here: 306 us
  Pallas kernels  292 us (95%)
  local copies, waits for them, and re-layouts  13.6 us (4%)
    pallas_call x1, Pallas kernels, local_attn(): pl.pallas_call(attn_kernel, out_shape=(jax.ShapeDtypeStruct((N_SEQ, 2, RO...  292 us
    transpose x2, local copies, waits for them, and re-layouts, join(): return jnp.transpose(x, (0, 2, 1, 3, 4)).reshape(N_SEQ, SHARD, 4, HEAD)  12.1 us

profile of v2, /device:TPU:0, one launch (start us, length us, event | category | flops | bytes accessed | tf_op | source)
XLA Modules:
  0.0 306.4 jit_solution(437868103889926006)
XLA Ops:
  0.6 292.2 %ctx_attn.1 = (bf16[4,2,2048,128]{3,2,1,0:T(8,128)(2,1)}, bf16[4,2,2048,128]{3,2,1,0:T(8,128)(2,1)}, bf16[2,4,1024,128]{3,2,1,0:T(8,128)(2,1)}) custom-call(bf16[4,1024,2,2,128]{4,3,2,1,0:T(2,128)(2,1)} %bitcast.20, bf16[4,1024,128]{2,1,0:T(8,128)(2,1)} %bitcast.26, bf16[4,1024,128]{2,1,0:T(8,128)(2,1)} %bitcast.27, bf16[4,1024,2,2,128]{4,3,2,1,0:T(2,128)(2,1)} %bitcast.21), custom_call_target="tpu_custom_call" | custom-call | tf_op jit(solution)/shard_map/ctx_attn/pallas_call | solution.py:374
  292.8 0.0 copy-start
  292.8 7.2 %copy.8 = bf16[4,1024,2,2,128]{4,3,2,1,0:T(2,128)(2,1)} copy(bf16[4,1024,2,2,128]{4,3,1,2,0:T(2,128)(2,1)} %bitcast.25) | data formatting | bytes 8388608 | tf_op jit(solution)/shard_map/transpose | solution.py:371
  300.1 0.0 copy-done
  300.1 0.0 copy-start.1
  300.1 4.9 %copy.9 = bf16[4,1024,2,2,128]{4,3,2,1,0:T(2,128)(2,1)} copy(bf16[4,1024,2,2,128]{4,3,1,2,0:T(2,128)(2,1)S(1)} %bitcast.24) | data formatting | bytes 8388608 | tf_op jit(solution)/shard_map/transpose | solution.py:371
  305.0 0.0 copy-done.1
  305.0 1.5 slice_bitcast_fusion
Async XLA Ops:
  292.8 7.2 %copy-start = (bf16[4,2,2048,128]{3,2,1,0:T(8,128)(2,1)S(1)}, bf16[4,2,2048,128]{3,2,1,0:T(8,128)(2,1)}, u32[]{:S(2)}) copy-start(bf16[4,2,2048,128]{3,2,1,0:T(8,128)(2,1)} %get-tuple-element.8) | copy-start | bytes 12582916
  300.1 4.9 %copy-start.1 = (bf16[2,4,1024,128]{3,2,1,0:T(8,128)(2,1)S(1)}, bf16[2,4,1024,128]{3,2,1,0:T(8,128)(2,1)}, u32[]{:S(2)}) copy-start(bf16[2,4,1024,128]{3,2,1,0:T(8,128)(2,1)} %get-tuple-element.9) | copy-start | bytes 6291460

commit v3 on v2

--- a/solution.py
+++ b/solution.py
@@ -55,11 +55,12 @@
 
     def arrival(n):
         u = n // 2
-        own = (3 - u) // 3
-        rel = (u * (3 - u)) // 2 * (1 + n % 2) + 3 * (n // 6)
+        near = (u * (3 - u)) // 2
         late = n // 4 - n // 6
-        cidx = n % 2 + late * (1 - 2 * (n % 2))
-        return chip_at(rel) * 2 + own * ((core + n) % 2) + (1 - own) * cidx
+        far = n // 6
+        bit = (core + n % 2) % 2
+        rel = near * ((1 - late) * (1 + bit) + late * (2 - bit)) + 3 * far
+        return chip_at(rel) * 2 + (1 - far) * bit + far * (n % 2)
 
     def departure(n):
         u = n // 2
@@ -107,19 +108,26 @@
     for what in range(2):
         kv_copy(what, mate, me).start()
     row_copy(2, mate, me).start()
-    def send_kvq(rel):
+    def send_kv(rel):
         for what in range(2):
             kv_copy(what, chip_at(rel) * 2 + what, me).start()
-        for cidx in range(2):
-            row_copy(2, chip_at(rel) * 2 + cidx, me).start()
+
+    def send_q(rel):
+        for flip in range(2):
+            row_copy(2, chip_at(rel) * 2 + (core + flip) % 2, me).start()
+
+    def send_kvq(rel):
+        send_kv(rel)
+        send_q(rel)
 
     def send_do():
         row_copy(3, mate, me).start()
-        for rel in (3, 1, 2):
-            for cidx in range(2):
-                row_copy(3, chip_at(rel) * 2 + cidx, me).start()
-
-    send_kvq(1 + core)
+        for rel in (3, 1 + core):
+            for flip in range(2):
+                row_copy(3, chip_at(rel) * 2 + (core + flip) % 2, me).start()
+        row_copy(3, chip_at(2 - core) * 2 + 1 - core, me).start()
+
+    send_kv(1 + core)
 
     def turn(land, dst, shard):
         for c in range(N_SUB):
@@ -127,16 +135,51 @@
             dst[shard, :, pl.ds(c * SUB, SUB)] = blk.T
 
     def fwd_diag(i):
+        part_keys = SUB // 2
+
+        def scores(c):
+            rows = pl.ds(c * SUB, SUB)
+            last = dot(kv_buf[0, i, pl.ds(c * part_keys, part_keys), :], q_t[i, :, rows], NN)
+            if c == 0:
+                return None, last
+            return dot(kv_buf[0, i, pl.ds(0, c * part_keys), :], q_t[i, :, rows], NN), last
+
+        here = scores(0)
         for c in range(N_SUB):
+            following = scores(c + 1) if c + 1 < N_SUB else None
             rows = pl.ds(c * SUB, SUB)
-            nkeys = (c + 1) * (SUB // 2)
-            s_t = dot(kv_buf[0, i, pl.ds(0, nkeys), :], q_t[i, :, rows], NN)
-            s_t = causal(s_t, 0, c * (SUB // 2), -jnp.inf)
-            mx = jnp.max(s_t, axis=0, keepdims=True)
-            p_t = jnp.exp2((s_t - mx) * LOG2_SCALE)
+            first, last = here
+            last = causal(last, 0, 0, -jnp.inf)
+            mx = jnp.max(last, axis=0, keepdims=True)
+            if first is not None:
+                mx = jnp.maximum(mx, jnp.max(first, axis=0, keepdims=True))
+            p_t = jnp.exp2((last - mx) * LOG2_SCALE)
+            total = jnp.sum(p_t, axis=0, keepdims=True)
+            out = dot(kv_t[i, :, pl.ds(c * part_keys, part_keys)], p_t.astype(BF16), NN)
+            if first is not None:
+                p_t = jnp.exp2((first - mx) * LOG2_SCALE)
+                total += jnp.sum(p_t, axis=0, keepdims=True)
+                out += dot(kv_t[i, :, pl.ds(0, c * part_keys)], p_t.astype(BF16), NN)
             row_m[i, :, rows] = mx
-            row_l[i, :, rows] = jnp.sum(p_t, axis=0, keepdims=True)
-            acc_t[i, :, rows] = dot(kv_t[i, :, pl.ds(0, nkeys)], p_t.astype(BF16), NN)
+            row_l[i, :, rows] = total
+            acc_t[i, :, rows] = out
+            here = following
+
+    def pass_on(shard):
+        kv_direct(shard).wait_recv()
+        kv_pass(shard, core).start()
+
+    def beside_last(n):
+        @pl.when(n == 2)
+        def _():
+            send_kv(2 - core)
+            row_copy(3, chip_at(2 - core) * 2 + core, me).start()
+
+        @pl.when(n == 3)
+        def _():
+            pass_on(arrival(4))
+            pass_on(arrival(5))
+            send_q(2 - core)
 
     def fwd_pairs(new, n):
         def place(step):
@@ -163,6 +206,10 @@
             acc_t[i, :, rows] = out
 
         def two(step, carry):
+            @pl.when(step == (n - 1) * (N_SUB // 2))
+            def _():
+                beside_last(n)
+
             for slot in range(2):
                 now = step * 2 + slot
                 s_buf[1 - slot] = scores(jnp.minimum(now + 1, n * N_SUB - 1))
@@ -200,25 +247,31 @@
         kv_t[new] = kv_buf[1, new].T
         fwd_diag(new)
 
+        @pl.when(n == 4 + 4 * core)
+        def _():
+            send_kvq(3)
+
+        @pl.when(n == 5)
+        def _():
+            pass_on(arrival(6))
+
+            @pl.when(core == 1)
+            def _():
+                send_kvq(3)
+
+        @pl.when(n == 6)
+        def _():
+            pass_on(arrival(7))
+            send_do()
+
         fwd_pairs(new, n)
 
-        @pl.when((n > 0) & (n < N_DEV - 1))
-        def _():
-            following = (arrival(n + 1))
-            kv_direct(following).wait_recv()
-            kv_pass(following, core).start()
-
-        @pl.when(n == 1)
-        def _():
-            send_kvq(2 - core)
-
-        @pl.when(n == 3 + core)
-        def _():
-            send_kvq(3)
-
-        @pl.when(n == 5 - core)
-        def _():
-            send_do()
+        @pl.when(n == 0)
+        def _():
+            pass_on(arrival(2))
+            pass_on(arrival(3))
+            send_q(1 + core)
+
         return carry
     lax.fori_loop(0, N_DEV, fwd_loop, 0)
     for n in range(2, N_DEV):
@@ -323,8 +376,15 @@
         shard = departure(n)
         bwd_diag(shard)
 
-        def pair(t, carry):
-            other = departure(t)
+        @pl.when(n > 4)
+        def _():
+            finish_dkv(departure(n - 1))
+
+        def pair(back, carry):
+            t = N_DEV + n - back
+            u = t // 2
+            first = 1 - (n + 7) // 8
+            other = departure(t + first * core * ((u * (3 - u)) // 2) * (1 - 2 * (t % 2)))
 
             @pl.when(n == 0)
             def _():
@@ -340,7 +400,7 @@
             stage[shard, rows, :] = (acc_t[shard, :, rows] * SCALE).astype(BF16).T
         start_out(1, shard)
 
-        @pl.when(n > 0)
+        @pl.when((n > 0) & (n < 5))
         def _():
             finish_dkv(departure(n - 1))
         return carry
@@ -365,11 +425,26 @@
             out_copy(what, source, source).wait_recv()
 
 
+def join_kernel(o_in, dq_in, dkv_in, o_out, dq_out, dk_out, dv_out, rows, keys, get_sem, put_sem):
+    moves = []
+    for which, (src, dst) in enumerate(((o_in, o_out), (dq_in, dq_out))):
+        for seq in range(N_SEQ):
+            for pair in range(2):
+                moves.append((src.at[seq, pair], rows.at[which, seq, pair], dst.at[seq, :, pair]))
+    for which, dst in enumerate((dv_out, dk_out)):
+        moves.append((dkv_in.at[which], keys.at[which], dst))
+    gets = [pltpu.make_async_copy(src, mid, get_sem.at[n]) for n, (src, mid, dst) in enumerate(moves)]
+    puts = [pltpu.make_async_copy(mid, dst, put_sem.at[n]) for n, (src, mid, dst) in enumerate(moves)]
+    for get in gets:
+        get.start()
+    for get, put in zip(gets, puts):
+        get.wait()
+        put.start()
+    for put in puts:
+        put.wait()
+
+
 def local_attn(queries, key_seq, value_seq, out_grad):
-    def join(x):
-        x = x.reshape(N_SEQ, 2, SHARD, 2, HEAD)
-        return jnp.transpose(x, (0, 2, 1, 3, 4)).reshape(N_SEQ, SHARD, 4, HEAD)
-
     any_spec = pl.BlockSpec(memory_space=pl.ANY)
     o_x, dq_x, dkv_x = pl.pallas_call(
         attn_kernel,
@@ -409,9 +484,23 @@
         name='ctx_attn',
     )(queries.reshape(N_SEQ, SHARD, 2, 2, HEAD), key_seq.reshape(N_SEQ, SHARD, HEAD),
       value_seq.reshape(N_SEQ, SHARD, HEAD), out_grad.reshape(N_SEQ, SHARD, 2, 2, HEAD))
-    k_grad = dkv_x[1].reshape(key_seq.shape)
-    v_grad = dkv_x[0].reshape(value_seq.shape)
-    return join(o_x), join(dq_x), k_grad, v_grad
+    rows_shape = jax.ShapeDtypeStruct((N_SEQ, SHARD, 2, 2, HEAD), BF16)
+    keys_shape = jax.ShapeDtypeStruct((N_SEQ, SHARD, HEAD), BF16)
+    attn_out, q_grad, k_grad, v_grad = pl.pallas_call(
+        join_kernel,
+        out_shape=(rows_shape, rows_shape, keys_shape, keys_shape),
+        in_specs=[any_spec] * 3,
+        out_specs=[any_spec] * 4,
+        scratch_shapes=[
+            pltpu.VMEM((2, N_SEQ, 2, SHARD, 2, HEAD), BF16),
+            pltpu.VMEM((2, N_SEQ, SHARD, HEAD), BF16),
+            pltpu.SemaphoreType.DMA((18,)),
+            pltpu.SemaphoreType.DMA((18,)),
+        ],
+        name='join_heads',
+    )(o_x.reshape(N_SEQ, 2, SHARD, 2, HEAD), dq_x.reshape(N_SEQ, 2, SHARD, 2, HEAD), dkv_x)
+    return (attn_out.reshape(queries.shape), q_grad.reshape(queries.shape),
+            k_grad.reshape(key_seq.shape), v_grad.reshape(value_seq.shape))
 
 
 def solution(mesh):

time: 307 us -> 288 us (0.938)
  local copies, waits for them, and re-layouts: 13.6 us -> 0 us
  Pallas kernels: 292 us -> 287 us
    pallas_call x1, Pallas kernels: 292 us -> 279 us  [local_attn(): pl.pallas_call(attn_kernel, out_shape=(jax.ShapeDtypeStruct((N_SEQ, 2, RO...]
    transpose x2 -> x0, local copies, waits for them, and re-layouts: 12.1 us -> none  [join(): return jnp.transpose(x, (0, 2, 1, 3, 4)).reshape(N_SEQ, SHARD, 4, HEAD)]
    pallas_call x0 -> x1, Pallas kernels: none -> 8.21 us  [local_attn(): pl.pallas_call(join_kernel, out_shape=(rows_shape, rows_shape, keys_shape...]
where the time goes in v3:
time: 288 us
  Pallas kernels  287 us (100%)
    pallas_call x1, Pallas kernels, local_attn(): pl.pallas_call(attn_kernel, out_shape=(jax.ShapeDtypeStruct((N_SEQ, 2, RO...  279 us
    pallas_call x1, Pallas kernels, local_attn(): pl.pallas_call(join_kernel, out_shape=(rows_shape, rows_shape, keys_shape...  8.21 us

profile of v3, /device:TPU:0, one launch (start us, length us, event | category | flops | bytes accessed | tf_op | source)
XLA Modules:
  0.0 287.8 jit_solution(8684462453676383368)
XLA Ops:
  0.6 279.0 %ctx_attn.1 = (bf16[4,2,2048,128]{3,2,1,0:T(8,128)(2,1)}, bf16[4,2,2048,128]{3,2,1,0:T(8,128)(2,1)}, bf16[2,4,1024,128]{3,2,1,0:T(8,128)(2,1)}) custom-call(bf16[4,1024,2,2,128]{4,3,2,1,0:T(2,128)(2,1)} %bitcast.14, bf16[4,1024,128]{2,1,0:T(8,128)(2,1)} %bitcast.18, bf16[4,1024,128]{2,1,0:T(8,128)(2,1)} %bitcast.19, bf16[4,1024,2,2,128]{4,3,2,1,0:T(2,128)(2,1)} %bitcast.15), custom_call_target="tpu_custom_call" | custom-call | tf_op jit(solution)/shard_map/ctx_attn/pallas_call | solution.py:449
  279.6 8.2 %join_heads.1 = (bf16[4,1024,2,2,128]{4,3,2,1,0:T(2,128)(2,1)}, bf16[4,1024,2,2,128]{4,3,2,1,0:T(2,128)(2,1)}, bf16[4,1024,128]{2,1,0:T(8,128)(2,1)}, bf16[4,1024,128]{2,1,0:T(8,128)(2,1)}) custom-call(bf16[4,2,1024,2,128]{4,3,2,1,0:T(2,128)(2,1)} %bitcast.16, bf16[4,2,1024,2,128]{4,3,2,1,0:T(2,128)(2,1)} %bitcast.17, ...), custom_call_target="tpu_custom_call" | custom-call | tf_op jit(solution)/shard_map/join_heads/pallas_call | solution.py:489

commit v4 on v3

--- a/solution.py
+++ b/solution.py
@@ -182,17 +182,16 @@
             send_q(2 - core)
 
     def fwd_pairs(new, n):
-        def place(step):
-            old = arrival(step // N_SUB)
-            return jnp.maximum(new, old), jnp.minimum(new, old), pl.ds(pl.multiple_of(step % N_SUB * SUB, SUB), SUB)
-
-        def scores(step):
-            i, j, rows = place(step)
-            return dot(kv_buf[0, j], q_t[i, :, rows], NN)
-
-        def softmax(step, slot):
-            i, j, rows = place(step)
-            s_t = s_buf[slot]
+        def pair_of(t):
+            old = arrival(t)
+            return jnp.maximum(new, old), jnp.minimum(new, old)
+
+        def scores(i, j, c):
+            return dot(kv_buf[0, j], q_t[i, :, pl.ds(c * SUB, SUB)], NN)
+
+        def softmax(i, j, c):
+            rows = pl.ds(c * SUB, SUB)
+            s_t = s_buf[c % 2]
             old = row_m[i, :, rows]
             mx = jnp.maximum(old, jnp.max(s_t, axis=0, keepdims=True))
             keep = jnp.exp2((old - mx) * LOG2_SCALE)
@@ -205,21 +204,22 @@
             row_l[i, :, rows] = total
             acc_t[i, :, rows] = out
 
-        def two(step, carry):
-            @pl.when(step == (n - 1) * (N_SUB // 2))
+        def pair(t, carry):
+            @pl.when(t == n - 1)
             def _():
                 beside_last(n)
 
-            for slot in range(2):
-                now = step * 2 + slot
-                s_buf[1 - slot] = scores(jnp.minimum(now + 1, n * N_SUB - 1))
-                softmax(now, slot)
+            i, j = pair_of(t)
+            i_next, j_next = pair_of(jnp.minimum(t + 1, n - 1))
+            for c in range(N_SUB):
+                s_buf[(c + 1) % 2] = scores(i, j, c + 1) if c + 1 < N_SUB else scores(i_next, j_next, 0)
+                softmax(i, j, c)
             return carry
 
         @pl.when(n > 0)
         def _():
-            s_buf[0] = scores(0)
-            lax.fori_loop(0, n * (N_SUB // 2), two, 0)
+            s_buf[0] = scores(*pair_of(0), 0)
+            lax.fori_loop(0, n, pair, 0)
 
     def fwd_loop(n, carry):
         new = arrival(n)
@@ -353,11 +353,8 @@
             bwd_block(i, c * SUB, i, (c + 1) * (SUB // 2), c * (SUB // 2), c % 2)
 
     def bwd_full(i, j):
-        def two(c, carry):
-            for slot in range(2):
-                bwd_block(i, pl.multiple_of(c * (2 * SUB) + slot * SUB, SUB), j, SHARD, None, slot)
-            return carry
-        lax.fori_loop(0, N_SUB // 2, two, 0)
+        for c in range(N_SUB):
+            bwd_block(i, c * SUB, j, SHARD, None, c % 2)
 
     def part_copy(shard):
         return pltpu.make_async_remote_copy(

time: 288 us -> 283 us (0.983)
  Pallas kernels: 287 us -> 282 us
    pallas_call x1, Pallas kernels: 279 us -> 274 us  [local_attn(): pl.pallas_call(attn_kernel, out_shape=(jax.ShapeDtypeStruct((N_SEQ, 2, RO...]
where the time goes in v4:
time: 283 us
  Pallas kernels  282 us (100%)
    pallas_call x1, Pallas kernels, local_attn(): pl.pallas_call(attn_kernel, out_shape=(jax.ShapeDtypeStruct((N_SEQ, 2, RO...  274 us
    pallas_call x1, Pallas kernels, local_attn(): pl.pallas_call(join_kernel, out_shape=(rows_shape, rows_shape, keys_shape...  8.21 us

profile of v4, /device:TPU:0, one launch (start us, length us, event | category | flops | bytes accessed | tf_op | source)
XLA Modules:
  0.0 282.6 jit_solution(2086276909726847634)
XLA Ops:
  0.6 273.6 %ctx_attn.1 = (bf16[4,2,2048,128]{3,2,1,0:T(8,128)(2,1)}, bf16[4,2,2048,128]{3,2,1,0:T(8,128)(2,1)}, bf16[2,4,1024,128]{3,2,1,0:T(8,128)(2,1)}) custom-call(bf16[4,1024,2,2,128]{4,3,2,1,0:T(2,128)(2,1)} %bitcast.14, bf16[4,1024,128]{2,1,0:T(8,128)(2,1)} %bitcast.18, bf16[4,1024,128]{2,1,0:T(8,128)(2,1)} %bitcast.19, bf16[4,1024,2,2,128]{4,3,2,1,0:T(2,128)(2,1)} %bitcast.15), custom_call_target="tpu_custom_call" | custom-call | tf_op jit(solution)/shard_map/ctx_attn/pallas_call | solution.py:446
  274.3 8.2 %join_heads.1 = (bf16[4,1024,2,2,128]{4,3,2,1,0:T(2,128)(2,1)}, bf16[4,1024,2,2,128]{4,3,2,1,0:T(2,128)(2,1)}, bf16[4,1024,128]{2,1,0:T(8,128)(2,1)}, bf16[4,1024,128]{2,1,0:T(8,128)(2,1)}) custom-call(bf16[4,2,1024,2,128]{4,3,2,1,0:T(2,128)(2,1)} %bitcast.16, bf16[4,2,1024,2,128]{4,3,2,1,0:T(2,128)(2,1)} %bitcast.17, ...), custom_call_target="tpu_custom_call" | custom-call | tf_op jit(solution)/shard_map/join_heads/pallas_call | solution.py:486
